TPU v7x, 32 devices: a whole 2x2x4 slice. The times are simulated.
32 devices in a mesh: rows: 8 (over z, x), cols: 4 (over y, core).
Axes of the slice: x: 2, y: 2, z: 4, core: 2. Of those that a mesh axis runs over, the one named last changes fastest.
Arguments:
- basis: float32 [65536, 256], P(('rows', 'cols')), may hold values from -8 to 8, as said below
- new_vectors: float32 [65536, 128], P(('rows', 'cols')), may hold values from -180 to 180
- jacobian: float32 [65536, 1024], P(('rows', 'cols')), may hold values from -0.1875 to 0.1875
Outputs:
- merged: float32 [65536, 384], P(('rows', 'cols'))
Inputs may be any that keep to these rules, and one draw needn't show every extreme that they name: The stored basis is orthonormal under the inner product divided by 65536 up to a drift of orthogonality: basis^T basis / 65536 differs from the identity by about 0.1 to 0.3 in spectral norm.
All inputs are finite; a program needn't handle non-finite values.
Results may differ from a plain program's by a relative error of at most 0.00005.
Values sent between devices are 32-bit elements; how exact they have to be, the bound alone decides.
No kernel may reach another device: no remote copies, remote signals or barrier semaphores. Data moves between devices by JAX's collectives and lax.ppermute only.
A program may use at most 64 MiB of HBM per device.

v0:
```python
import jax
import jax.numpy as jnp
from jax import lax
from jax.experimental import pallas as pl
from jax.experimental.pallas import tpu as pltpu
from jax.sharding import PartitionSpec as P

F32 = jnp.float32
BF16 = jnp.bfloat16
LANES = 128
BLOCK = 16
VMEM = pltpu.MemorySpace.VMEM


def halves(value):
    high = value.astype(BF16)
    return high, (value - high.astype(F32)).astype(BF16)


def thirds(value):
    high = value.astype(BF16)
    rest = value - high.astype(F32)
    middle = rest.astype(BF16)
    return high, middle, (rest - middle.astype(F32)).astype(BF16)


def contract(left, right, left_dim, right_dim):
    return lax.dot_general(
        left, right, (((left_dim,), (right_dim,)), ((), ())), preferred_element_type=F32
    )


def three(left, right, left_dim, right_dim):
    return (
        contract(left[0], right[0], left_dim, right_dim)
        + contract(left[0], right[1], left_dim, right_dim)
        + contract(left[1], right[0], left_dim, right_dim)
    )


def exact(left, right, left_dim, right_dim):
    return lax.dot_general(
        left,
        right,
        (((left_dim,), (right_dim,)), ((), ())),
        precision=lax.Precision.HIGHEST,
        preferred_element_type=F32,
    )


def products_kernel(which_ref, basis_ref, new_ref, jac_ref, out_ref):
    step = pl.program_id(0)

    @pl.when(step == 0)
    def _():
        out_ref[...] = jnp.zeros_like(out_ref)

    shards = out_ref.shape[0]
    wide = basis_ref.shape[1] + new_ref.shape[1]
    lane = jac_ref.shape[1] // shards
    stacked = halves(jnp.concatenate([basis_ref[...], new_ref[...]], axis=1))
    jac = halves(jac_ref[...])
    prod = three(stacked, jac, 0, 0)
    for s in range(shards):
        out_ref[s, :wide, :] += prod[:, s * lane : (s + 1) * lane]
    tiles = wide // LANES
    pairs = [(i, j) for i in range(tiles) for j in range(i, tiles)]
    half = len(pairs) // 2
    piece = out_ref.shape[1] - wide

    def tile(index):
        return tuple(part[:, index * LANES : (index + 1) * LANES] for part in stacked)

    def gram(which):
        def run():
            blocks = [three(tile(i), tile(j), 0, 0) for i, j in pairs[which * half : (which + 1) * half]]
            rows = jnp.concatenate(blocks, axis=0)
            for s in range(shards):
                out_ref[s, wide:, :] += rows[s * piece : (s + 1) * piece]

        return run

    pl.when(which_ref[0] == 0)(gram(0))
    pl.when(which_ref[0] == 1)(gram(1))


def products(which, basis, new_vectors, jacobian):
    rows, width = basis.shape
    block = new_vectors.shape[1]
    wide = width + block
    obs = jacobian.shape[1]
    tiles = wide // LANES
    packed = tiles * (tiles + 1) // 2 * LANES
    chunk = rows // 4
    return pl.pallas_call(
        products_kernel,
        grid_spec=pltpu.PrefetchScalarGridSpec(
            num_scalar_prefetch=1,
            grid=(rows // chunk,),
            in_specs=[
                pl.BlockSpec((chunk, width), lambda k, w: (k, 0)),
                pl.BlockSpec((chunk, block), lambda k, w: (k, 0)),
                pl.BlockSpec((chunk, obs // 2), lambda k, w: (k, w[0])),
            ],
            out_specs=pl.BlockSpec((4, wide + packed // 8, obs // 8), lambda k, w: (0, 0, 0)),
        ),
        out_shape=jax.ShapeDtypeStruct((4, wide + packed // 8, obs // 8), F32),
    )(which, basis, new_vectors, jacobian)


def factor(m_ref):
    n = m_ref.shape[0]
    tiles = n // LANES
    for phase in range(tiles):
        base = LANES * phase

        def step(k, carry, base=base):
            start = base + k * BLOCK
            mine = pl.ds(pl.multiple_of(start, BLOCK), BLOCK)
            rows = m_ref[mine, :]
            diag = rows[:, base : base + LANES]
            row = lax.broadcasted_iota(jnp.int32, (BLOCK, LANES), 0)
            cols = [
                jnp.take_along_axis(diag, jnp.full((BLOCK, LANES), k * BLOCK + q, jnp.int32), axis=1)
                for q in range(BLOCK)
            ]
            lane = lax.broadcasted_iota(jnp.int32, (BLOCK, n), 1) - start
            sub = lax.broadcasted_iota(jnp.int32, (BLOCK, n), 0)
            unit = jnp.where(lane == sub, 1.0, 0.0)
            work = jnp.where((lane >= 0) & (lane < BLOCK), unit, rows)
            parts = [work[:, t * LANES : (t + 1) * LANES] for t in range(tiles)]
            pivots = jnp.ones((BLOCK, LANES), F32)
            for p in range(BLOCK):
                pivot = jnp.broadcast_to(cols[p][p : p + 1, :], (BLOCK, LANES))
                pivots = jnp.where(row == p, pivot, pivots)
                if p + 1 < BLOCK:
                    mult = jnp.where(row > p, cols[p], 0.0) * (1.0 / pivot)
                    for q in range(p + 1, BLOCK):
                        cols[q] = cols[q] - mult * jnp.broadcast_to(cols[q][p : p + 1, :], (BLOCK, LANES))
                    parts = [x - mult * jnp.broadcast_to(x[p : p + 1, :], (BLOCK, LANES)) for x in parts]
            inv = lax.rsqrt(pivots)
            done = jnp.concatenate([x * inv for x in parts], axis=1)
            rest = jnp.where(lane >= BLOCK, done, 0.0)[:, base:]
            h, m, l = thirds(done)
            hr, mr, lr = thirds(rest)
            right = jnp.concatenate([h, m, h, l, h, m, l, m], axis=0)
            left = jnp.concatenate([hr, hr, mr, hr, lr, mr, mr, lr], axis=0)
            update = contract(left, right, 0, 0)
            lanes = lax.broadcasted_iota(jnp.int32, (n - base, n), 1) - start
            keep = (lanes < 0) | (lanes >= BLOCK)
            m_ref[base:, :] = jnp.where(keep, m_ref[base:, :], 0.0) - update
            m_ref[mine, :] = done
            return carry

        lax.fori_loop(0, LANES // BLOCK, step, 0)


def whiten_kernel(width, scale, gram_ref, hess_ref, out_ref):
    n = out_ref.shape[0]
    tiles = n // LANES
    pairs = [(i, j) for i in range(tiles) for j in range(i, tiles)]

    def whole(ref):
        blocks = {}
        for index, (i, j) in enumerate(pairs):
            value = ref[index * LANES : (index + 1) * LANES, :] * scale
            blocks[i, j] = value
            if i != j:
                blocks[j, i] = value.T
        return jnp.concatenate(
            [jnp.concatenate([blocks[i, j] for j in range(tiles)], axis=1) for i in range(tiles)], axis=0
        )

    full = whole(gram_ref)
    hess = whole(hess_ref)
    s_vv, s_vw, s_ww = full[:width, :width], full[:width, width:], full[width:, width:]
    second = s_vw - exact(s_vv, s_vw, 1, 0)
    summed = s_vw + second
    gram = s_ww - exact(summed, s_vw, 0, 0) - exact(s_vw, summed, 0, 0)
    gram = gram + exact(summed, exact(s_vv, summed, 1, 0), 0, 0)
    corner = exact(summed, summed, 0, 0) + gram
    r = lax.broadcasted_iota(jnp.int32, (width, width), 0)
    c = lax.broadcasted_iota(jnp.int32, (width, width), 1)
    out_ref[:width, :width] = hess[:width, :width] + jnp.where(r == c, 1.0, 0.0)
    out_ref[:width, width:] = hess[:width, width:] + summed
    out_ref[width:, :width] = hess[width:, :width] + summed.T
    out_ref[width:, width:] = hess[width:, width:] + corner
    factor(out_ref)
    r = lax.broadcasted_iota(jnp.int32, (n, n), 0)
    c = lax.broadcasted_iota(jnp.int32, (n, n), 1)
    out_ref[...] = jnp.where(r >= c, out_ref[...], 0.0)


def whiten(width, n, scale, gram, hess):
    def kernel(gram_ref, hess_ref, out_ref):
        whiten_kernel(width, scale, gram_ref, hess_ref, out_ref)

    return pl.pallas_call(
        kernel,
        in_specs=[pl.BlockSpec(memory_space=VMEM)] * 2,
        out_specs=pl.BlockSpec(memory_space=VMEM),
        out_shape=jax.ShapeDtypeStruct((n, n), F32),
    )(gram, hess)


def apply_kernel(basis_ref, new_ref, inv_ref, out_ref):
    width = basis_ref.shape[1]
    old = halves(basis_ref[...])
    new = halves(new_ref[...])
    inv = halves(inv_ref[...])
    top = tuple(x[:width, :width] for x in inv)
    left = tuple(x[width:, :width] for x in inv)
    corner = tuple(x[width:, width:] for x in inv)
    out_ref[:, :width] = three(old, top, 1, 1)
    out_ref[:, width:] = three(old, left, 1, 1) + three(new, corner, 1, 1)


def apply(basis, new_vectors, inv):
    rows, width = basis.shape
    block = new_vectors.shape[1]
    wide = width + block
    chunk = rows // 4
    return pl.pallas_call(
        apply_kernel,
        grid=(rows // chunk,),
        in_specs=[
            pl.BlockSpec((chunk, width), lambda k: (k, 0)),
            pl.BlockSpec((chunk, block), lambda k: (k, 0)),
            pl.BlockSpec((wide, wide), lambda k: (0, 0)),
        ],
        out_specs=pl.BlockSpec((chunk, wide), lambda k: (k, 0)),
        out_shape=jax.ShapeDtypeStruct((rows, wide), F32),
    )(basis, new_vectors, inv)


def swap(value, axis, mask):
    size = lax.axis_size(axis)
    return lax.ppermute(value, axis, [(i, i ^ mask) for i in range(size)])


def pick(value, index, dim):
    return lax.dynamic_index_in_dim(value, index, dim, keepdims=False)


def ordered(bit, own, other):
    return jnp.stack([jnp.where(bit == 0, own, other), jnp.where(bit == 0, other, own)])


def local(basis, new_vectors, jacobian):
    n_rows, n_cols = lax.axis_size("rows"), lax.axis_size("cols")
    total = basis.shape[0] * n_rows * n_cols
    width = basis.shape[1]
    wide = width + new_vectors.shape[1]
    at_row, at_col = lax.axis_index("rows"), lax.axis_index("cols")
    c, y, x = at_col & 1, (at_col >> 1) & 1, at_row & 1
    rest = [("cols", 1 << b) for b in range(2, n_cols.bit_length() - 1)]
    rest += [("rows", m) for m in (2, 6) if m < n_rows]
    rest += [("rows", 1 << b) for b in range(3, n_rows.bit_length() - 1)]

    theirs = products((1 - c).reshape(1), basis, new_vectors, jacobian)
    got = swap(theirs, "cols", 1)
    mine = products(c.reshape(1), basis, new_vectors, jacobian)
    both = (mine + got).reshape(2, 2, *mine.shape[1:])
    cut = both.shape[2] // 2
    a, b = both[:, :, :cut], both[:, :, cut:]
    got_a = swap(pick(a, 1 - y, 0), "cols", 2)
    got_b = swap(pick(b, 1 - x, 1), "rows", 1)
    a = pick(a, y, 0) + got_a
    b = pick(b, x, 1) + got_b
    got_a = swap(pick(a, 1 - x, 0), "rows", 1)
    got_b = swap(pick(b, 1 - y, 0), "cols", 2)
    a = pick(a, x, 0) + got_a
    b = pick(b, y, 0) + got_b
    for (axis_a, mask_a), (axis_b, mask_b) in zip(rest, rest[::-1]):
        got_a = swap(a, axis_a, mask_a)
        got_b = swap(b, axis_b, mask_b)
        a, b = a + got_a, b + got_b
    shard = jnp.concatenate([a, b], axis=0)
    proj, gram = shard[:wide], shard[wide:]

    tiles = wide // LANES
    hess = exact(proj, proj, 1, 1)
    hess = jnp.concatenate(
        [
            hess[i * LANES : (i + 1) * LANES, j * LANES : (j + 1) * LANES]
            for i in range(tiles)
            for j in range(i, tiles)
        ],
        axis=0,
    ).reshape(2, -1, LANES)
    hess = pick(hess, c, 0) + swap(pick(hess, 1 - c, 0), "cols", 1)
    cut = hess.shape[0] // 2
    h_a, h_b = hess[:cut], hess[cut:]
    g_cut = gram.shape[0] // 2
    g_a, g_b = gram[:g_cut], gram[g_cut:]
    got_a = swap(jnp.concatenate([h_a, g_a]), "cols", 2)
    got_b = swap(jnp.concatenate([h_b, g_b]), "rows", 1)
    h_a, h_b = h_a + got_a[:cut], h_b + got_b[:cut]
    g_a = ordered(y, g_a, got_a[cut:])
    g_b = ordered(x, g_b, got_b[cut:])
    got_a = swap(jnp.concatenate([h_a, g_a.reshape(-1, LANES)]), "rows", 1)
    got_b = swap(jnp.concatenate([h_b, g_b.reshape(-1, LANES)]), "cols", 2)
    h_a, h_b = h_a + got_a[:cut], h_b + got_b[:cut]
    g_a = ordered(x, g_a, got_a[cut:].reshape(g_a.shape))
    g_b = ordered(y, g_b, got_b[cut:].reshape(g_b.shape))
    gram = jnp.concatenate([jnp.swapaxes(g_a, 0, 1), g_b], axis=2).reshape(-1, LANES)
    hess = jnp.concatenate([h_a, h_b])
    send = jnp.stack([hess, gram])
    full = ordered(c, send, swap(send, "cols", 1))
    hess = full[:, 0].reshape(-1, LANES)
    gram = full[:, 1].reshape(-1, LANES)
    inv = whiten(width, wide, 1.0 / total, gram, hess)
    return apply(basis, new_vectors, inv)


def solution(mesh):
    placed = (P(("rows", "cols"), None), P(("rows", "cols"), None), P(("rows", "cols"), None))
    return jax.shard_map(
        local, mesh=mesh, in_specs=placed, out_specs=P(("rows", "cols"), None), check_vma=False
    )
```

profile of v0, /device:TPU:0, one launch (start us, length us, event | category | flops | bytes accessed | tf_op | source)
XLA Modules:
  0.0 88.2 jit_solution(16004425382850771923)
XLA Ops:
  0.0 7.9 %shard_map.38 = f32[4,480,128]{2,1,0:T(8,128)} custom-call(s32[1]{0:T(128)} %bitcast.1.which_ref, f32[2048,256]{1,0:T(8,128)} %basis_ref.5, f32[2048,128]{1,0:T(8,128)} %new_ref.5, f32[2048,1024]{1,0:T(8,128)} %jac_ref.3), custom_call_target="tpu_custom_call" | custom-call | tf_op jit(solution)/shard_map/pallas_call | solution.py:95
  7.9 0.5 collective-permute-start
  8.4 7.9 %shard_map.37 = f32[4,480,128]{2,1,0:T(8,128)} custom-call(s32[1]{0:T(128)} %bitcast.which_ref, f32[2048,256]{1,0:T(8,128)} %basis_ref.5, f32[2048,128]{1,0:T(8,128)} %new_ref.5, f32[2048,1024]{1,0:T(8,128)} %jac_ref.3), custom_call_target="tpu_custom_call" | custom-call | tf_op jit(solution)/shard_map/pallas_call | solution.py:95
  16.2 0.0 collective-permute-done
  16.2 1.3 %add.71 = f32[4,480,128]{2,1,0:T(8,128)S(1)} add(f32[4,480,128]{2,1,0:T(8,128)} %shard_map.37, f32[4,480,128]{2,1,0:T(8,128)S(1)} %collective-permute-done) | non-fusion elementwise | flops 245760 | bytes 2949120 | tf_op jit(solution)/shard_map/add | solution.py:263
  17.5 0.1 fusion.16
  17.7 2.5 %collective-permute-start.5 = (f32[2,240,128]{2,1,0:T(8,128)S(1)}, f32[2,240,128]{2,1,0:T(8,128)S(1)}, u32[]{:S(2)}, u32[]{:S(2)}) collective-permute-start(f32[2,240,128]{2,1,0:T(8,128)S(1)} %dynamic-slice_bitcast_fusion), channel_id=1, source_target_pairs={{0,4},{4,0},{8,12},{12,8},{16,20},{20,16},{24,28},{28,24},{1,5},{5... | collective-permute-start | bytes 737288 | tf_op jit(solution)/shard_map/ppermute | solution.py:238
  20.2 1.6 %collective-permute-start.1 = (f32[2,240,128]{2,1,0:T(8,128)S(1)}, f32[2,240,128]{2,1,0:T(8,128)S(1)}, u32[]{:S(2)}, u32[]{:S(2)}) collective-permute-start(f32[2,240,128]{2,1,0:T(8,128)S(1)} %dynamic-slice_bitcast_fusion.1), channel_id=1, source_target_pairs={{0,2},{1,3},{2,0},{3,1},{4,6},{5,7},{6,4},{7,5},{8,10},{9,11},{10,... | collective-permute-start | bytes 737288 | tf_op jit(solution)/shard_map/ppermute | solution.py:238
  21.8 5.0 %collective-permute-done.5 = f32[2,240,128]{2,1,0:T(8,128)S(1)} collective-permute-done((f32[2,240,128]{2,1,0:T(8,128)S(1)}, f32[2,240,128]{2,1,0:T(8,128)S(1)}, u32[]{:S(2)}, u32[]{:S(2)}) %collective-permute-start.5) | collective-permute-done | bytes 245792 | tf_op jit(solution)/shard_map/ppermute | solution.py:238
  26.9 1.8 %collective-permute-start.6 = (f32[240,128]{1,0:T(8,128)S(1)}, f32[240,128]{1,0:T(8,128)S(1)}, u32[]{:S(2)}, u32[]{:S(2)}) collective-permute-start(f32[240,128]{1,0:T(8,128)S(1)} %dynamic-slice_bitcast_fusion.3), channel_id=1, source_target_pairs={{0,2},{1,3},{2,0},{3,1},{4,6},{5,7},{6,4},{7,5},{8,10},{9,11},{10,... | collective-permute-start | bytes 368648 | tf_op jit(solution)/shard_map/ppermute | solution.py:238
  28.7 0.0 collective-permute-done.1
  28.8 1.6 %collective-permute-start.2 = (f32[240,128]{1,0:T(8,128)S(1)}, f32[240,128]{1,0:T(8,128)S(1)}, u32[]{:S(2)}, u32[]{:S(2)}) collective-permute-start(f32[240,128]{1,0:T(8,128)S(1)} %dynamic-slice_bitcast_fusion.4), channel_id=1, source_target_pairs={{0,4},{4,0},{8,12},{12,8},{16,20},{20,16},{24,28},{28,24},{1,5},{5... | collective-permute-start | bytes 368648 | tf_op jit(solution)/shard_map/ppermute | solution.py:238
  30.3 1.7 %collective-permute-done.6 = f32[240,128]{1,0:T(8,128)S(1)} collective-permute-done((f32[240,128]{1,0:T(8,128)S(1)}, f32[240,128]{1,0:T(8,128)S(1)}, u32[]{:S(2)}, u32[]{:S(2)}) %collective-permute-start.6) | collective-permute-done | bytes 122912 | tf_op jit(solution)/shard_map/ppermute | solution.py:238
  32.1 3.7 %collective-permute-start.7 = (f32[240,128]{1,0:T(8,128)S(1)}, f32[240,128]{1,0:T(8,128)S(1)}, u32[]{:S(2)}, u32[]{:S(2)}) collective-permute-start(f32[240,128]{1,0:T(8,128)S(1)} %bitcast_add_fusion.3), channel_id=1, source_target_pairs={{0,24},{4,28},{8,16},{12,20},{16,8},{20,12},{24,0},{28,4},{1,25},{... | collective-permute-start | bytes 368648 | tf_op jit(solution)/shard_map/ppermute | solution.py:238
  35.7 0.0 collective-permute-done.2
  35.8 0.1 collective-permute-start.3
  35.8 3.7 %collective-permute-done.7 = f32[240,128]{1,0:T(8,128)S(1)} collective-permute-done((f32[240,128]{1,0:T(8,128)S(1)}, f32[240,128]{1,0:T(8,128)S(1)}, u32[]{:S(2)}, u32[]{:S(2)}) %collective-permute-start.7) | collective-permute-done | bytes 122912 | tf_op jit(solution)/shard_map/ppermute | solution.py:238
  39.6 0.1 collective-permute-start.8
  39.6 2.5 %collective-permute-done.3 = f32[240,128]{1,0:T(8,128)S(1)} collective-permute-done((f32[240,128]{1,0:T(8,128)S(1)}, f32[240,128]{1,0:T(8,128)S(1)}, u32[]{:S(2)}, u32[]{:S(2)}) %collective-permute-start.3) | collective-permute-done | bytes 122912 | tf_op jit(solution)/shard_map/ppermute | solution.py:238
  42.2 2.3 %collective-permute-start.4 = (f32[240,128]{1,0:T(8,128)S(1)}, f32[240,128]{1,0:T(8,128)S(1)}, u32[]{:S(2)}, u32[]{:S(2)}) collective-permute-start(f32[240,128]{1,0:T(8,128)S(1)} %add.78), channel_id=1, source_target_pairs={{0,24},{4,28},{8,16},{12,20},{16,8},{20,12},{24,0},{28,4},{1,25},{... | collective-permute-start | bytes 368648 | tf_op jit(solution)/shard_map/ppermute | solution.py:238
  44.4 1.4 %collective-permute-done.8 = f32[240,128]{1,0:T(8,128)S(1)} collective-permute-done((f32[240,128]{1,0:T(8,128)S(1)}, f32[240,128]{1,0:T(8,128)S(1)}, u32[]{:S(2)}, u32[]{:S(2)}) %collective-permute-start.8) | collective-permute-done | bytes 122912 | tf_op jit(solution)/shard_map/ppermute | solution.py:238
  45.8 3.2 %collective-permute-done.4 = f32[240,128]{1,0:T(8,128)S(1)} collective-permute-done((f32[240,128]{1,0:T(8,128)S(1)}, f32[240,128]{1,0:T(8,128)S(1)}, u32[]{:S(2)}, u32[]{:S(2)}) %collective-permute-start.4) | collective-permute-done | bytes 122912 | tf_op jit(solution)/shard_map/ppermute | solution.py:238
  49.0 0.6 fusion.1
  49.8 0.1 collective-permute-start.9
  49.9 1.4 %collective-permute-done.9 = f32[384,128]{1,0:T(8,128)S(1)} collective-permute-done((f32[384,128]{1,0:T(8,128)S(1)}, f32[384,128]{1,0:T(8,128)S(1)}, u32[]{:S(2)}, u32[]{:S(2)}) %collective-permute-start.9) | collective-permute-done | bytes 196640 | tf_op jit(solution)/shard_map/ppermute | solution.py:238
  51.4 1.5 %collective-permute-start.12 = (f32[240,128]{1,0:T(8,128)S(1)}, f32[240,128]{1,0:T(8,128)S(1)}, u32[]{:S(2)}, u32[]{:S(2)}) collective-permute-start(f32[240,128]{1,0:T(8,128)S(1)} %pad_maximum_fusion.7), channel_id=1, source_target_pairs={{0,4},{4,0},{8,12},{12,8},{16,20},{20,16},{24,28},{28,24},{1,5},{5... | collective-permute-start | bytes 368648 | tf_op jit(solution)/shard_map/ppermute | solution.py:238
  52.9 1.3 %collective-permute-start.10 = (f32[240,128]{1,0:T(8,128)S(1)}, f32[240,128]{1,0:T(8,128)S(1)}, u32[]{:S(2)}, u32[]{:S(2)}) collective-permute-start(f32[240,128]{1,0:T(8,128)S(1)} %pad_maximum_fusion.6), channel_id=1, source_target_pairs={{0,2},{1,3},{2,0},{3,1},{4,6},{5,7},{6,4},{7,5},{8,10},{9,11},{10,... | collective-permute-start | bytes 368648 | tf_op jit(solution)/shard_map/ppermute | solution.py:238
  54.3 2.5 %collective-permute-done.12 = f32[240,128]{1,0:T(8,128)S(1)} collective-permute-done((f32[240,128]{1,0:T(8,128)S(1)}, f32[240,128]{1,0:T(8,128)S(1)}, u32[]{:S(2)}, u32[]{:S(2)}) %collective-permute-start.12) | collective-permute-done | bytes 122912 | tf_op jit(solution)/shard_map/ppermute | solution.py:238
  56.8 1.3 %collective-permute-done.10 = f32[240,128]{1,0:T(8,128)S(1)} collective-permute-done((f32[240,128]{1,0:T(8,128)S(1)}, f32[240,128]{1,0:T(8,128)S(1)}, u32[]{:S(2)}, u32[]{:S(2)}) %collective-permute-start.10) | collective-permute-done | bytes 122912 | tf_op jit(solution)/shard_map/ppermute | solution.py:238
  58.2 0.6 collective-permute-start.11
  58.8 1.3 %collective-permute-start.13 = (f32[288,128]{1,0:T(8,128)S(1)}, f32[288,128]{1,0:T(8,128)S(1)}, u32[]{:S(2)}, u32[]{:S(2)}) collective-permute-start(f32[288,128]{1,0:T(8,128)S(1)} %pad_maximum_fusion.5), channel_id=1, source_target_pairs={{0,2},{1,3},{2,0},{3,1},{4,6},{5,7},{6,4},{7,5},{8,10},{9,11},{10,... | collective-permute-start | bytes 442376 | tf_op jit(solution)/shard_map/ppermute | solution.py:238
  60.1 3.2 %collective-permute-done.11 = f32[288,128]{1,0:T(8,128)S(1)} collective-permute-done((f32[288,128]{1,0:T(8,128)S(1)}, f32[288,128]{1,0:T(8,128)S(1)}, u32[]{:S(2)}, u32[]{:S(2)}) %collective-permute-start.11) | collective-permute-done | bytes 147488 | tf_op jit(solution)/shard_map/ppermute | solution.py:238
  63.4 0.6 collective-permute-done.13
  64.1 0.1 collective-permute-start.14
  64.2 1.7 %collective-permute-done.14 = f32[2,384,128]{2,1,0:T(8,128)S(1)} collective-permute-done((f32[2,384,128]{2,1,0:T(8,128)S(1)}, f32[2,384,128]{2,1,0:T(8,128)S(1)}, u32[]{:S(2)}, u32[]{:S(2)}) %collective-permute-start.14) | collective-permute-done | bytes 393248 | tf_op jit(solution)/shard_map/ppermute | solution.py:238
  65.9 0.1 select_bitcast_fusion
  66.0 0.9 %pad_maximum_fusion = (f32[2,1,384,128]{3,2,0,1:T(8,128)}, f32[2,1,384,128]{3,2,0,1:T(8,128)}) fusion(f32[1,2,384,128]{3,2,0,1:T(8,128)S(1)} %get-tuple-element.9, f32[1,2,384,128]{3,2,0,1:T(8,128)S(1)} %get-tuple-element.10), kind=kLoop, calls=%fused_computation.3 | loop fusion | flops 196608 | bytes 1572864 | tf_op jit(solution)/shard_map/stack | solution.py:246
  66.9 15.6 %shard_map.39.inv_ref = f32[384,384]{1,0:T(8,128)} custom-call(f32[768,128]{1,0:T(8,128)} %bitcast.63, f32[768,128]{1,0:T(8,128)} %bitcast.62), custom_call_target="tpu_custom_call" | custom-call | tf_op jit(solution)/shard_map/pallas_call | solution.py:198
  82.5 5.7 %shard_map.40 = f32[2048,384]{1,0:T(8,128)} custom-call(f32[2048,256]{1,0:T(8,128)} %basis_ref.5, f32[2048,128]{1,0:T(8,128)} %new_ref.5, f32[384,384]{1,0:T(8,128)} %shard_map.39.inv_ref), custom_call_target="tpu_custom_call" | custom-call | tf_op jit(solution)/shard_map/pallas_call | solution.py:223
  (38 shorter events, 0.6 us)
Async XLA Ops:
  7.9 8.4 %collective-permute-start = (f32[4,480,128]{2,1,0:T(8,128)}, f32[4,480,128]{2,1,0:T(8,128)S(1)}, u32[]{:S(2)}, u32[]{:S(2)}) collective-permute-start(f32[4,480,128]{2,1,0:T(8,128)} %shard_map.38), channel_id=1, source_target_pairs={{0,1},{1,0},{2,3},{3,2},{4,5},{5,4},{6,7},{7,6},{8,9},{9,8},{10,11... | collective-permute-start | bytes 2949128 | tf_op jit(solution)/shard_map/ppermute | solution.py:238
  17.7 9.1 %collective-permute-start.5 = (f32[2,240,128]{2,1,0:T(8,128)S(1)}, f32[2,240,128]{2,1,0:T(8,128)S(1)}, u32[]{:S(2)}, u32[]{:S(2)}) collective-permute-start(f32[2,240,128]{2,1,0:T(8,128)S(1)} %dynamic-slice_bitcast_fusion), channel_id=1, source_target_pairs={{0,4},{4,0},{8,12},{12,8},{16,20},{20,16},{24,28},{28,24},{1,5},{5... | collective-permute-start | bytes 737288 | tf_op jit(solution)/shard_map/ppermute | solution.py:238
  20.2 8.5 %collective-permute-start.1 = (f32[2,240,128]{2,1,0:T(8,128)S(1)}, f32[2,240,128]{2,1,0:T(8,128)S(1)}, u32[]{:S(2)}, u32[]{:S(2)}) collective-permute-start(f32[2,240,128]{2,1,0:T(8,128)S(1)} %dynamic-slice_bitcast_fusion.1), channel_id=1, source_target_pairs={{0,2},{1,3},{2,0},{3,1},{4,6},{5,7},{6,4},{7,5},{8,10},{9,11},{10,... | collective-permute-start | bytes 737288 | tf_op jit(solution)/shard_map/ppermute | solution.py:238
  26.9 5.2 %collective-permute-start.6 = (f32[240,128]{1,0:T(8,128)S(1)}, f32[240,128]{1,0:T(8,128)S(1)}, u32[]{:S(2)}, u32[]{:S(2)}) collective-permute-start(f32[240,128]{1,0:T(8,128)S(1)} %dynamic-slice_bitcast_fusion.3), channel_id=1, source_target_pairs={{0,2},{1,3},{2,0},{3,1},{4,6},{5,7},{6,4},{7,5},{8,10},{9,11},{10,... | collective-permute-start | bytes 368648 | tf_op jit(solution)/shard_map/ppermute | solution.py:238
  28.8 7.0 %collective-permute-start.2 = (f32[240,128]{1,0:T(8,128)S(1)}, f32[240,128]{1,0:T(8,128)S(1)}, u32[]{:S(2)}, u32[]{:S(2)}) collective-permute-start(f32[240,128]{1,0:T(8,128)S(1)} %dynamic-slice_bitcast_fusion.4), channel_id=1, source_target_pairs={{0,4},{4,0},{8,12},{12,8},{16,20},{20,16},{24,28},{28,24},{1,5},{5... | collective-permute-start | bytes 368648 | tf_op jit(solution)/shard_map/ppermute | solution.py:238
  32.1 7.5 %collective-permute-start.7 = (f32[240,128]{1,0:T(8,128)S(1)}, f32[240,128]{1,0:T(8,128)S(1)}, u32[]{:S(2)}, u32[]{:S(2)}) collective-permute-start(f32[240,128]{1,0:T(8,128)S(1)} %bitcast_add_fusion.3), channel_id=1, source_target_pairs={{0,24},{4,28},{8,16},{12,20},{16,8},{20,12},{24,0},{28,4},{1,25},{... | collective-permute-start | bytes 368648 | tf_op jit(solution)/shard_map/ppermute | solution.py:238
  35.8 6.4 %collective-permute-start.3 = (f32[240,128]{1,0:T(8,128)S(1)}, f32[240,128]{1,0:T(8,128)S(1)}, u32[]{:S(2)}, u32[]{:S(2)}) collective-permute-start(f32[240,128]{1,0:T(8,128)S(1)} %bitcast_add_fusion.4), channel_id=1, source_target_pairs={{0,8},{4,12},{8,0},{12,4},{16,24},{20,28},{24,16},{28,20},{1,9},{5... | collective-permute-start | bytes 368648 | tf_op jit(solution)/shard_map/ppermute | solution.py:238
  39.6 6.3 %collective-permute-start.8 = (f32[240,128]{1,0:T(8,128)S(1)}, f32[240,128]{1,0:T(8,128)S(1)}, u32[]{:S(2)}, u32[]{:S(2)}) collective-permute-start(f32[240,128]{1,0:T(8,128)S(1)} %add.82), channel_id=1, source_target_pairs={{0,8},{4,12},{8,0},{12,4},{16,24},{20,28},{24,16},{28,20},{1,9},{5... | collective-permute-start | bytes 368648 | tf_op jit(solution)/shard_map/ppermute | solution.py:238
  42.2 6.8 %collective-permute-start.4 = (f32[240,128]{1,0:T(8,128)S(1)}, f32[240,128]{1,0:T(8,128)S(1)}, u32[]{:S(2)}, u32[]{:S(2)}) collective-permute-start(f32[240,128]{1,0:T(8,128)S(1)} %add.78), channel_id=1, source_target_pairs={{0,24},{4,28},{8,16},{12,20},{16,8},{20,12},{24,0},{28,4},{1,25},{... | collective-permute-start | bytes 368648 | tf_op jit(solution)/shard_map/ppermute | solution.py:238
  49.8 1.5 %collective-permute-start.9 = (f32[384,128]{1,0:T(8,128)S(1)}, f32[384,128]{1,0:T(8,128)S(1)}, u32[]{:S(2)}, u32[]{:S(2)}) collective-permute-start(f32[384,128]{1,0:T(8,128)S(1)} %dynamic-slice_bitcast_fusion.2), channel_id=1, source_target_pairs={{0,1},{1,0},{2,3},{3,2},{4,5},{5,4},{6,7},{7,6},{8,9},{9,8},{10,11... | collective-permute-start | bytes 589832 | tf_op jit(solution)/shard_map/ppermute | solution.py:238
  51.4 5.4 %collective-permute-start.12 = (f32[240,128]{1,0:T(8,128)S(1)}, f32[240,128]{1,0:T(8,128)S(1)}, u32[]{:S(2)}, u32[]{:S(2)}) collective-permute-start(f32[240,128]{1,0:T(8,128)S(1)} %pad_maximum_fusion.7), channel_id=1, source_target_pairs={{0,4},{4,0},{8,12},{12,8},{16,20},{20,16},{24,28},{28,24},{1,5},{5... | collective-permute-start | bytes 368648 | tf_op jit(solution)/shard_map/ppermute | solution.py:238
  52.9 5.2 %collective-permute-start.10 = (f32[240,128]{1,0:T(8,128)S(1)}, f32[240,128]{1,0:T(8,128)S(1)}, u32[]{:S(2)}, u32[]{:S(2)}) collective-permute-start(f32[240,128]{1,0:T(8,128)S(1)} %pad_maximum_fusion.6), channel_id=1, source_target_pairs={{0,2},{1,3},{2,0},{3,1},{4,6},{5,7},{6,4},{7,5},{8,10},{9,11},{10,... | collective-permute-start | bytes 368648 | tf_op jit(solution)/shard_map/ppermute | solution.py:238
  58.2 5.2 %collective-permute-start.11 = (f32[288,128]{1,0:T(8,128)S(1)}, f32[288,128]{1,0:T(8,128)S(1)}, u32[]{:S(2)}, u32[]{:S(2)}) collective-permute-start(f32[288,128]{1,0:T(8,128)S(1)} %pad_maximum_fusion.4), channel_id=1, source_target_pairs={{0,4},{4,0},{8,12},{12,8},{16,20},{20,16},{24,28},{28,24},{1,5},{5... | collective-permute-start | bytes 442376 | tf_op jit(solution)/shard_map/ppermute | solution.py:238
  58.8 5.2 %collective-permute-start.13 = (f32[288,128]{1,0:T(8,128)S(1)}, f32[288,128]{1,0:T(8,128)S(1)}, u32[]{:S(2)}, u32[]{:S(2)}) collective-permute-start(f32[288,128]{1,0:T(8,128)S(1)} %pad_maximum_fusion.5), channel_id=1, source_target_pairs={{0,2},{1,3},{2,0},{3,1},{4,6},{5,7},{6,4},{7,5},{8,10},{9,11},{10,... | collective-permute-start | bytes 442376 | tf_op jit(solution)/shard_map/ppermute | solution.py:238
  64.1 1.8 %collective-permute-start.14 = (f32[2,384,128]{2,1,0:T(8,128)S(1)}, f32[2,384,128]{2,1,0:T(8,128)S(1)}, u32[]{:S(2)}, u32[]{:S(2)}) collective-permute-start(f32[2,384,128]{2,1,0:T(8,128)S(1)} %pad_maximum_fusion.1), channel_id=1, source_target_pairs={{0,1},{1,0},{2,3},{3,2},{4,5},{5,4},{6,7},{7,6},{8,9},{9,8},{10,11... | collective-permute-start | bytes 1179656 | tf_op jit(solution)/shard_map/ppermute | solution.py:238
where the time goes:
time: 88.6 us; the launch traced here: 88.2 us
  Pallas kernels  37.1 us (42%)
  waiting for transfers between devices  28.3 us (32%)
  starting transfers between devices  19.1 us (22%)
  other arithmetic  2.68 us (3%)
    ppermute x15, waiting for transfers between devices, swap(): return lax.ppermute(value, axis, [(i, i ^ mask) for i in range(size)])  28.3 us
    ppermute x15, starting transfers between devices, swap(): return lax.ppermute(value, axis, [(i, i ^ mask) for i in range(size)])  19.1 us
    pallas_call x2, Pallas kernels, products(): pl.pallas_call(products_kernel, grid_spec=pltpu.PrefetchScalarGridSpec(nu...  15.7 us
    pallas_call x1, Pallas kernels, whiten(): pl.pallas_call(kernel, in_specs=[pl.BlockSpec(memory_space=VMEM)] * 2, ou...  15.6 us
    pallas_call x1, Pallas kernels, apply(): pl.pallas_call(apply_kernel, grid=(rows // chunk,), in_specs=[pl.BlockSpe...  5.73 us
  transfers between devices with their start and end apart: 15, of which 12 were waited for; matrix products, arithmetic and copies ran while one was open for 0% of the time, Pallas kernels for 9%

commit v1 on v0

v1 whole, which is shorter than its diff:
```python
import functools

import jax
import jax.numpy as jnp
from jax import lax
from jax.experimental import pallas as pl
from jax.experimental.pallas import tpu as pltpu
from jax.sharding import PartitionSpec as P

F32 = jnp.float32
BF16 = jnp.bfloat16
LANES = 128
BLOCK = 16
CHUNKS = 4
LIMIT = pltpu.CompilerParams(vmem_limit_bytes=32 << 20)
VMEM = pltpu.VMEM


def halves(value):
    high = value.astype(BF16)
    return high, (value - high.astype(F32)).astype(BF16)


def thirds(value):
    high = value.astype(BF16)
    rest = value - high.astype(F32)
    middle = rest.astype(BF16)
    return high, middle, (rest - middle.astype(F32)).astype(BF16)


def contract(left, right, left_dim, right_dim):
    return lax.dot_general(
        left, right, (((left_dim,), (right_dim,)), ((), ())), preferred_element_type=F32
    )


def three(left, right, left_dim, right_dim):
    return (
        contract(left[0], right[0], left_dim, right_dim)
        + contract(left[0], right[1], left_dim, right_dim)
        + contract(left[1], right[0], left_dim, right_dim)
    )


def exact(left, right, left_dim, right_dim):
    return lax.dot_general(
        left,
        right,
        (((left_dim,), (right_dim,)), ((), ())),
        precision=lax.Precision.HIGHEST,
        preferred_element_type=F32,
    )


def spread(outs, value, extra):
    lanes = outs[0].shape[2]
    piece = extra.shape[0] // outs[0].shape[0]
    cut = outs[0].shape[1]
    tall = value.shape[0]
    for s in range(outs[0].shape[0]):
        tile = value[:, s * lanes : (s + 1) * lanes]
        outs[0][s, :, :] = tile[:cut]
        outs[1][s, : tall - cut, :] = tile[cut:]
        outs[1][s, tall - cut :, :] = extra[s * piece : (s + 1) * piece]


def products_kernel(first, core_ref, basis_ref, new_ref, jac_ref, *refs):
    if first:
        out_a_ref, out_b_ref, own_ref, vec_ref, obs_ref, sems = refs
    else:
        own_ref, out_a_ref, out_b_ref, vec_ref, obs_ref, sems = refs
    rows, width = basis_ref.shape
    wide = vec_ref.shape[1]
    part = obs_ref.shape[1]
    chunk = rows // CHUNKS
    index = 1 - core_ref[0] if first else core_ref[0]
    lanes = pl.ds(pl.multiple_of(index * part, part), part)

    def copies(k):
        at = pl.ds(k * chunk, chunk)
        return (
            pltpu.make_async_copy(basis_ref.at[at, :], vec_ref.at[at, pl.ds(0, width)], sems.at[k, 0]),
            pltpu.make_async_copy(new_ref.at[at, :], vec_ref.at[at, pl.ds(width, wide - width)], sems.at[k, 1]),
            pltpu.make_async_copy(jac_ref.at[at, lanes], obs_ref.at[at, :], sems.at[k, 2]),
        )

    for k in range(CHUNKS):
        for copy in copies(k):
            copy.start()
    total = None
    for k in range(CHUNKS):
        for copy in copies(k):
            copy.wait()
        at = slice(k * chunk, (k + 1) * chunk)
        value = vec_ref[at, :]
        flipped = halves(value.T)
        sums = [three(flipped, halves(obs_ref[at, :]), 1, 0)]
        if first:
            stacked = halves(value)
            sums += [contract(flipped[0], part, 1, 0) for part in stacked]
        total = sums if total is None else [x + y for x, y in zip(total, sums)]
    if not first:
        spread((out_a_ref, out_b_ref), total[0], own_ref[...])
        return
    prod, near, far = total
    gram = near + far + far.T
    tiles = wide // LANES
    blocks = [gram[i * LANES : (i + 1) * LANES, j * LANES : (j + 1) * LANES] for j in range(tiles) for i in range(j, tiles)]
    half = len(blocks) // 2
    low, high = (jnp.concatenate(blocks[k * half : (k + 1) * half], axis=0) for k in range(2))
    lead = core_ref[0] == 1
    spread((out_a_ref, out_b_ref), prod, jnp.where(lead, low, high))
    own_ref[...] = jnp.where(lead, high, low)


def products(core, basis, new_vectors, jacobian):
    rows, width = basis.shape
    wide = width + new_vectors.shape[1]
    obs = jacobian.shape[1]
    tiles = wide // LANES
    packed = tiles * (tiles + 1) // 2 * LANES // 8
    sums = VMEM((4, (wide + packed) // 2, obs // 8), F32)
    own = VMEM((4 * packed, obs // 8), F32)
    inside = pl.BlockSpec(memory_space=VMEM)
    outside = pl.BlockSpec(memory_space=pltpu.HBM)
    scalar = pl.BlockSpec(memory_space=pltpu.SMEM)

    def call(first, *more):
        return pl.pallas_call(
            functools.partial(products_kernel, first),
            in_specs=[scalar, outside, outside, outside] + [inside] * len(more),
            out_specs=[inside] * (3 if first else 2),
            out_shape=[sums, sums, own] if first else [sums, sums],
            scratch_shapes=[
                VMEM((rows, wide), F32),
                VMEM((rows, obs // 2), F32),
                pltpu.SemaphoreType.DMA((CHUNKS, 3)),
            ],
            compiler_params=LIMIT,
        )(core, basis, new_vectors, jacobian, *more)

    *theirs, own = call(True)
    return call(False, own), theirs


def factor(m_ref):
    n = m_ref.shape[0]
    tiles = n // LANES
    for phase in range(tiles):
        base = LANES * phase

        def step(k, carry, base=base):
            start = base + k * BLOCK
            mine = pl.ds(pl.multiple_of(start, BLOCK), BLOCK)
            rows = m_ref[mine, :]
            diag = rows[:, base : base + LANES]
            row = lax.broadcasted_iota(jnp.int32, (BLOCK, LANES), 0)
            cols = [
                jnp.take_along_axis(diag, jnp.full((BLOCK, LANES), k * BLOCK + q, jnp.int32), axis=1)
                for q in range(BLOCK)
            ]
            lane = lax.broadcasted_iota(jnp.int32, (BLOCK, n), 1) - start
            sub = lax.broadcasted_iota(jnp.int32, (BLOCK, n), 0)
            unit = jnp.where(lane == sub, 1.0, 0.0)
            work = jnp.where((lane >= 0) & (lane < BLOCK), unit, rows)
            parts = [work[:, t * LANES : (t + 1) * LANES] for t in range(tiles)]
            pivots = jnp.ones((BLOCK, LANES), F32)
            for p in range(0, BLOCK, 2):
                base_row = (p + 1) // 8 * 8

                def wide_row(value, index, low=base_row):
                    return jnp.broadcast_to(value[index : index + 1, :], (BLOCK - low, LANES))

                a, b, c = wide_row(cols[p], p, 0), wide_row(cols[p], p + 1, 0), wide_row(cols[p + 1], p + 1, 0)
                det = a * c - b * b
                over_det, over_a = 1.0 / det, 1.0 / a
                pivots = jnp.where(row == p, a, jnp.where(row == p + 1, det * over_a, pivots))
                under = row[base_row:] > p + 1
                x, y = cols[p][base_row:], cols[p + 1][base_row:]
                a, b, c, ratio, over_det = (v[base_row:] for v in (a, b, c, b * over_a, over_det))
                mult = jnp.where(under, (x * c - y * b) * over_det, 0.0)
                next_mult = jnp.where(under, (y * a - x * b) * over_det, 0.0)

                def cleared(value, first_mult, p=p, low=base_row, next_mult=next_mult, wide_row=wide_row):
                    new = value[low:] - first_mult * wide_row(value, p) - next_mult * wide_row(value, p + 1)
                    return jnp.concatenate([value[:low], new], axis=0) if low else new

                for q in range(p + 2, BLOCK):
                    cols[q] = cleared(cols[q], mult)
                mult = jnp.where(row[base_row:] == p + 1, ratio, mult)
                parts = [cleared(value, mult) for value in parts]
            inv = lax.rsqrt(pivots)
            done = jnp.concatenate([x * inv for x in parts], axis=1)
            rest = jnp.where(lane >= BLOCK, done, 0.0)[:, base:]
            h, m, l = thirds(done)
            hr, mr, lr = thirds(rest)
            right = jnp.concatenate([h, m, h, l, h, m, l, m], axis=0)
            left = jnp.concatenate([hr, hr, mr, hr, lr, mr, mr, lr], axis=0)
            update = contract(left, right, 0, 0)
            lanes = lax.broadcasted_iota(jnp.int32, (n - base, n), 1) - start
            keep = (lanes < 0) | (lanes >= BLOCK)
            m_ref[base:, :] = jnp.where(keep, m_ref[base:, :], 0.0) - update
            m_ref[mine, :] = done
            return carry

        lax.fori_loop(0, LANES // BLOCK, step, 0)


def hess_kernel(core_ref, a_ref, got_a_ref, b_ref, got_b_ref, keep_a_ref, keep_b_ref, give_a_ref, give_b_ref, gram_a_ref, gram_b_ref):
    shard = jnp.concatenate([a_ref[...] + got_a_ref[...], b_ref[...] + got_b_ref[...]], axis=0)
    cut = gram_a_ref.shape[0]
    wide = shard.shape[0] - 2 * cut
    tiles = wide // LANES
    hess = exact(shard[:wide], shard[:wide], 1, 1)
    blocks = [
        hess[i * LANES : (i + 1) * LANES, j * LANES : (j + 1) * LANES] for j in range(tiles) for i in range(j, tiles)
    ]
    half = len(blocks) // 2
    first, second = (jnp.concatenate(blocks[k * half : (k + 1) * half], axis=0) for k in range(2))
    lead = core_ref[0] == 1
    keep, give = jnp.where(lead, second, first), jnp.where(lead, first, second)
    middle = keep_a_ref.shape[0]
    keep_a_ref[...], keep_b_ref[...] = keep[:middle], keep[middle:]
    give_a_ref[...], give_b_ref[...] = give[:middle], give[middle:]
    gram_a_ref[...], gram_b_ref[...] = shard[wide : wide + cut], shard[wide + cut :]


def shard_hess(core, wide, a, got_a, b, got_b):
    inside = pl.BlockSpec(memory_space=VMEM)
    tiles = wide // LANES
    part = VMEM((tiles * (tiles + 1) * LANES // 8, LANES), F32)
    gram = VMEM(((2 * a.shape[0] - wide) // 2, LANES), F32)
    return pl.pallas_call(
        hess_kernel,
        in_specs=[pl.BlockSpec(memory_space=pltpu.SMEM)] + [inside] * 4,
        out_specs=[inside] * 6,
        out_shape=[part] * 4 + [gram] * 2,
        compiler_params=LIMIT,
    )(core, a, got_a, b, got_b)


def whiten_kernel(scale, lead_ref, own_ref, got_ref, basis_ref, new_ref, out_ref, m_ref, vec_ref, res_ref, sems):
    n = m_ref.shape[0]
    rows, width = basis_ref.shape
    chunk = rows // CHUNKS

    def loads(k):
        at = pl.ds(k * chunk, chunk)
        return (
            pltpu.make_async_copy(basis_ref.at[at, :], vec_ref.at[at, pl.ds(0, width)], sems.at[k, 0]),
            pltpu.make_async_copy(new_ref.at[at, :], vec_ref.at[at, pl.ds(width, n - width)], sems.at[k, 1]),
        )

    for k in range(CHUNKS):
        for copy in loads(k):
            copy.start()
    tiles = n // LANES
    pairs = [(i, j) for j in range(tiles) for i in range(j, tiles)]
    half = len(pairs) // 2
    lead = lead_ref[0] == 1

    def whole(which):
        blocks = {}
        for index, (i, j) in enumerate(pairs):
            rest = index % half * LANES
            at = slice(rest, rest + LANES)
            value = jnp.where(lead == (index >= half), own_ref[which, at, :], got_ref[which, at, :]) * scale
            blocks[i, j] = value
            if i != j:
                blocks[j, i] = value.T
        return jnp.concatenate(
            [jnp.concatenate([blocks[i, j] for j in range(tiles)], axis=1) for i in range(tiles)], axis=0
        )

    hess = whole(0)
    full = whole(1)
    s_vv, s_vw, s_ww = full[:width, :width], full[:width, width:], full[width:, width:]
    second = s_vw - exact(s_vv, s_vw, 1, 0)
    summed = s_vw + second
    gram = s_ww - exact(summed, s_vw, 0, 0) - exact(s_vw, summed, 0, 0)
    gram = gram + exact(summed, exact(s_vv, summed, 1, 0), 0, 0)
    corner = exact(summed, summed, 0, 0) + gram
    r = lax.broadcasted_iota(jnp.int32, (width, width), 0)
    c = lax.broadcasted_iota(jnp.int32, (width, width), 1)
    m_ref[:width, :width] = hess[:width, :width] + jnp.where(r == c, 1.0, 0.0)
    m_ref[:width, width:] = hess[:width, width:] + summed
    m_ref[width:, :width] = hess[width:, :width] + summed.T
    m_ref[width:, width:] = hess[width:, width:] + corner
    factor(m_ref)
    r = lax.broadcasted_iota(jnp.int32, (n, n), 0)
    c = lax.broadcasted_iota(jnp.int32, (n, n), 1)
    mix = halves(jnp.where(r >= c, m_ref[...], 0.0).T)
    corner = tuple(x[:width, :width] for x in mix)
    last = tuple(x[:, width:] for x in mix)

    def store(k):
        at = pl.ds(k * chunk, chunk)
        return pltpu.make_async_copy(res_ref.at[at, :], out_ref.at[at, :], sems.at[k, 2])

    for k in range(CHUNKS):
        at = slice(k * chunk, (k + 1) * chunk)
        for copy in loads(k):
            copy.wait()
        value = halves(vec_ref[at, :])
        old = tuple(x[:, :width] for x in value)
        res_ref[at, :width] = three(old, corner, 1, 0)
        res_ref[at, width:] = three(value, last, 1, 0)
        store(k).start()
    for k in range(CHUNKS):
        store(k).wait()


def whiten(scale, lead, own, got, basis, new_vectors):
    rows, width = basis.shape
    n = width + new_vectors.shape[1]

    def kernel(*refs):
        whiten_kernel(scale, *refs)

    inside = pl.BlockSpec(memory_space=VMEM)
    outside = pl.BlockSpec(memory_space=pltpu.HBM)
    return pl.pallas_call(
        kernel,
        in_specs=[pl.BlockSpec(memory_space=pltpu.SMEM), inside, inside, outside, outside],
        out_specs=outside,
        out_shape=jax.ShapeDtypeStruct((rows, n), F32),
        scratch_shapes=[
            VMEM((n, n), F32),
            VMEM((rows, n), F32),
            VMEM((rows, n), F32),
            pltpu.SemaphoreType.DMA((CHUNKS, 3)),
        ],
        compiler_params=LIMIT,
    )(lead, own, got, basis, new_vectors)


def pick(value, index):
    return lax.dynamic_index_in_dim(value, index, 0, keepdims=False)


def ordered(bit, own, other):
    return jnp.stack([jnp.where(bit == 0, own, other), jnp.where(bit == 0, other, own)])


def swap(value, axis, mask):
    size = lax.axis_size(axis)
    return lax.ppermute(value, axis, [(i, i ^ mask) for i in range(size)])


def local(basis, new_vectors, jacobian):
    n_rows, n_cols = lax.axis_size("rows"), lax.axis_size("cols")
    total = basis.shape[0] * n_rows * n_cols
    wide = basis.shape[1] + new_vectors.shape[1]
    at_row, at_col = lax.axis_index("rows"), lax.axis_index("cols")
    core, y, x = (at_col & 1).reshape(1), (at_col >> 1) & 1, at_row & 1
    rest = [("cols", 1 << b) for b in range(2, n_cols.bit_length() - 1)]
    rest += [("rows", m) for m in (2, 6) if m < n_rows]
    rest += [("rows", 1 << b) for b in range(3, n_rows.bit_length() - 1)]

    basis, new_vectors, jacobian = (
        pltpu.with_memory_space_constraint(value, pltpu.HBM) for value in (basis, new_vectors, jacobian)
    )
    mine, theirs = products(core, basis, new_vectors, jacobian)
    a, b = (value.reshape(2, 2, *value.shape[1:]) for value in mine)
    up_a, up_b = (swap(value, "cols", 1).reshape(a.shape) for value in theirs)

    def across(value, index):
        return lax.dynamic_index_in_dim(value, index, 1, keepdims=False)

    def both(value, up, got, at_y, at_x, index):
        return pick(pick(value, at_y), at_x) + pick(pick(up, at_y), at_x) + pick(got, index)

    got_a = swap(pick(a, 1 - y) + pick(up_a, 1 - y), "cols", 2)
    got_b = swap(across(b, 1 - x) + across(up_b, 1 - x), "rows", 1)
    next_a = swap(both(a, up_a, got_a, y, 1 - x, 1 - x), "rows", 1)
    next_b = swap(both(b, up_b, got_b, 1 - y, x, 1 - y), "cols", 2)
    a, got_a = both(a, up_a, got_a, y, x, x), next_a
    b, got_b = both(b, up_b, got_b, y, x, y), next_b
    for (axis_a, mask_a), (axis_b, mask_b) in zip(rest, rest[::-1]):
        a, b = a + got_a, b + got_b
        got_a = swap(a, axis_a, mask_a)
        got_b = swap(b, axis_b, mask_b)

    keep_a, keep_b, give_a, give_b, g_a, g_b = shard_hess(core, wide, a, got_a, b, got_b)
    h_a, h_b = keep_a + swap(give_a, "cols", 1), keep_b + swap(give_b, "cols", 1)
    cut = h_a.shape[0]
    got_a = swap(jnp.concatenate([h_a, g_a]), "cols", 2)
    got_b = swap(jnp.concatenate([h_b, g_b]), "rows", 1)
    h_a, h_b = h_a + got_a[:cut], h_b + got_b[:cut]
    g_a = ordered(y, g_a, got_a[cut:])
    g_b = ordered(x, g_b, got_b[cut:])
    got_a = swap(jnp.concatenate([h_a, g_a.reshape(-1, LANES)]), "rows", 1)
    got_b = swap(jnp.concatenate([h_b, g_b.reshape(-1, LANES)]), "cols", 2)
    h_a, h_b = h_a + got_a[:cut], h_b + got_b[:cut]
    g_a = ordered(x, g_a, got_a[cut:].reshape(g_a.shape))
    g_b = ordered(y, g_b, got_b[cut:].reshape(g_b.shape))
    gram = jnp.concatenate([jnp.swapaxes(g_a, 0, 1), g_b], axis=2).reshape(-1, LANES)
    own = jnp.stack([jnp.concatenate([h_a, h_b]), gram])
    return whiten(1.0 / total, core, own, swap(own, "cols", 1), basis, new_vectors)


def solution(mesh):
    placed = (P(("rows", "cols"), None), P(("rows", "cols"), None), P(("rows", "cols"), None))
    return jax.shard_map(
        local, mesh=mesh, in_specs=placed, out_specs=P(("rows", "cols"), None), check_vma=False
    )
```

time: 88.6 us -> 74.7 us (0.84)
  waiting for transfers between devices: 28.3 us -> 18.3 us
  Pallas kernels: 37.1 us -> 28.6 us
  starting transfers between devices: 19.1 us -> 26.7 us
  other arithmetic: 2.68 us -> 0.45 us
    ppermute x15 -> x17, waiting for transfers between devices: 28.3 us -> 18.3 us  [swap(): return lax.ppermute(value, axis, [(i, i ^ mask) for i in range(size)])]
    pallas_call x4, Pallas kernels: 37.1 us -> 28.6 us  [the longest x1 17.2 us: whiten(): pl.pallas_call(kernel, in_specs=[pl.BlockSpec(memory_space=pltpu.SMEM), i...]
    ppermute x15 -> x17, starting transfers between devices: 19.1 us -> 26.7 us  [swap(): return lax.ppermute(value, axis, [(i, i ^ mask) for i in range(size)])]
    add x6, other arithmetic: 1.41 us -> 0.13 us  [the longest x2 0.04 us: both(): pick(pick(value, at_y), at_x) + pick(pick(up, at_y), at_x)]
    another operation x4, other arithmetic: 1.01 us -> 0.04 us  [ordered(): jnp.stack([jnp.where(bit == 0, own, other), jnp.where(bit == 0, other, ow...]
  transfers between devices with their start and end apart: 15 -> 17, of which waited for: 12 -> 10; matrix products, arithmetic and copies ran while one was open for 0% -> 0% of each run, Pallas kernels for 9% -> 6%
where the time goes in v1:
time: 74.7 us; the launch traced here: 74.5 us
  Pallas kernels  28.6 us (38%)
  starting transfers between devices  26.7 us (36%)
  waiting for transfers between devices  18.3 us (24%)
    ppermute x17, starting transfers between devices, swap(): return lax.ppermute(value, axis, [(i, i ^ mask) for i in range(size)])  26.7 us
    ppermute x17, waiting for transfers between devices, swap(): return lax.ppermute(value, axis, [(i, i ^ mask) for i in range(size)])  18.3 us
    pallas_call x1, Pallas kernels, whiten(): pl.pallas_call(kernel, in_specs=[pl.BlockSpec(memory_space=pltpu.SMEM), i...  17.2 us
    pallas_call x2, Pallas kernels, call(): pl.pallas_call(functools.partial(products_kernel, first), in_specs=[scala...  10.8 us
  transfers between devices with their start and end apart: 17, of which 10 were waited for; matrix products, arithmetic and copies ran while one was open for 0% of the time, Pallas kernels for 6%

profile of v1, /device:TPU:0, one launch (start us, length us, event | category | flops | bytes accessed | tf_op | source)
XLA Modules:
  0.0 74.5 jit_solution(3286718437652236731)
XLA Ops:
  0.0 6.3 %shard_map.37 = (f32[4,240,128]{2,1,0:T(8,128)S(1)}, f32[4,240,128]{2,1,0:T(8,128)S(1)}, f32[384,128]{1,0:T(8,128)S(1)}) custom-call(s32[1]{0:T(128)} %bitcast.core_ref.refs_0_, f32[2048,256]{1,0:T(8,128)} %refs_3_.1, f32[2048,128]{1,0:T(8,128)} %refs_4_.1, f32[2048,1024]{1,0:T(8,128)} %jac_ref.3), custom_call_target="tpu_custom_call" | custom-call | tf_op jit(solution)/shard_map/pallas_call | solution.py:129
  6.3 0.6 collective-permute-start
  6.9 0.1 collective-permute-start.5
  7.0 4.5 %shard_map.38 = (f32[4,240,128]{2,1,0:T(8,128)S(1)}, f32[4,240,128]{2,1,0:T(8,128)S(1)}) custom-call(s32[1]{0:T(128)} %bitcast.core_ref.refs_0_, f32[2048,256]{1,0:T(8,128)} %refs_3_.1, f32[2048,128]{1,0:T(8,128)} %refs_4_.1, f32[2048,1024]{1,0:T(8,128)} %jac_ref.3, f32[384,128]{1,0:T(8,128)S(1)} %get-tuple-element.16.refs_0_), custom_call_target="tpu_custom_call" | custom-call | tf_op jit(solution)/shard_map/pallas_call | solution.py:129
  11.5 0.0 collective-permute-done
  11.5 3.0 %collective-permute-start.1 = (f32[2,240,128]{2,1,0:T(8,128)S(1)}, f32[2,240,128]{2,1,0:T(8,128)S(1)}, u32[]{:S(2)}, u32[]{:S(2)}) collective-permute-start(f32[2,240,128]{2,1,0:T(8,128)S(1)} %add_bitcast_fusion.1), channel_id=1, source_target_pairs={{0,2},{1,3},{2,0},{3,1},{4,6},{5,7},{6,4},{7,5},{8,10},{9,11},{10,... | collective-permute-start | bytes 737288 | tf_op jit(solution)/shard_map/ppermute | solution.py:347
  14.5 0.0 collective-permute-done.5
  14.6 1.6 %collective-permute-start.6 = (f32[2,240,128]{2,1,0:T(8,128)S(1)}, f32[2,240,128]{2,1,0:T(8,128)S(1)}, u32[]{:S(2)}, u32[]{:S(2)}) collective-permute-start(f32[2,240,128]{2,1,0:T(8,128)S(1)} %add_bitcast_fusion), channel_id=1, source_target_pairs={{0,4},{4,0},{8,12},{12,8},{16,20},{20,16},{24,28},{28,24},{1,5},{5... | collective-permute-start | bytes 737288 | tf_op jit(solution)/shard_map/ppermute | solution.py:347
  16.1 4.6 %collective-permute-done.1 = f32[2,240,128]{2,1,0:T(8,128)S(1)} collective-permute-done((f32[2,240,128]{2,1,0:T(8,128)S(1)}, f32[2,240,128]{2,1,0:T(8,128)S(1)}, u32[]{:S(2)}, u32[]{:S(2)}) %collective-permute-start.1) | collective-permute-done | bytes 245792 | tf_op jit(solution)/shard_map/ppermute | solution.py:347
  20.8 1.8 %collective-permute-start.2 = (f32[240,128]{1,0:T(8,128)S(1)}, f32[240,128]{1,0:T(8,128)S(1)}, u32[]{:S(2)}, u32[]{:S(2)}) collective-permute-start(f32[240,128]{1,0:T(8,128)S(1)} %bitcast_add_fusion.2), channel_id=1, source_target_pairs={{0,4},{4,0},{8,12},{12,8},{16,20},{20,16},{24,28},{28,24},{1,5},{5... | collective-permute-start | bytes 368648 | tf_op jit(solution)/shard_map/ppermute | solution.py:347
  22.5 0.0 collective-permute-done.6
  22.6 1.6 %collective-permute-start.7 = (f32[240,128]{1,0:T(8,128)S(1)}, f32[240,128]{1,0:T(8,128)S(1)}, u32[]{:S(2)}, u32[]{:S(2)}) collective-permute-start(f32[240,128]{1,0:T(8,128)S(1)} %bitcast_add_fusion), channel_id=1, source_target_pairs={{0,2},{1,3},{2,0},{3,1},{4,6},{5,7},{6,4},{7,5},{8,10},{9,11},{10,... | collective-permute-start | bytes 368648 | tf_op jit(solution)/shard_map/ppermute | solution.py:347
  24.1 1.6 %collective-permute-done.2 = f32[240,128]{1,0:T(8,128)S(1)} collective-permute-done((f32[240,128]{1,0:T(8,128)S(1)}, f32[240,128]{1,0:T(8,128)S(1)}, u32[]{:S(2)}, u32[]{:S(2)}) %collective-permute-start.2) | collective-permute-done | bytes 122912 | tf_op jit(solution)/shard_map/ppermute | solution.py:347
  25.7 1.9 %collective-permute-start.3 = (f32[240,128]{1,0:T(8,128)S(1)}, f32[240,128]{1,0:T(8,128)S(1)}, u32[]{:S(2)}, u32[]{:S(2)}) collective-permute-start(f32[240,128]{1,0:T(8,128)S(1)} %fusion.1), channel_id=1, source_target_pairs={{0,8},{4,12},{8,0},{12,4},{16,24},{20,28},{24,16},{28,20},{1,9},{5... | collective-permute-start | bytes 368648 | tf_op jit(solution)/shard_map/ppermute | solution.py:347
  27.6 0.0 collective-permute-done.7
  27.6 3.6 %collective-permute-start.8 = (f32[240,128]{1,0:T(8,128)S(1)}, f32[240,128]{1,0:T(8,128)S(1)}, u32[]{:S(2)}, u32[]{:S(2)}) collective-permute-start(f32[240,128]{1,0:T(8,128)S(1)} %fusion), channel_id=1, source_target_pairs={{0,24},{4,28},{8,16},{12,20},{16,8},{20,12},{24,0},{28,4},{1,25},{... | collective-permute-start | bytes 368648 | tf_op jit(solution)/shard_map/ppermute | solution.py:347
  31.2 0.8 %collective-permute-done.3 = f32[240,128]{1,0:T(8,128)S(1)} collective-permute-done((f32[240,128]{1,0:T(8,128)S(1)}, f32[240,128]{1,0:T(8,128)S(1)}, u32[]{:S(2)}, u32[]{:S(2)}) %collective-permute-start.3) | collective-permute-done | bytes 122912 | tf_op jit(solution)/shard_map/ppermute | solution.py:347
  32.0 3.9 %collective-permute-start.4 = (f32[240,128]{1,0:T(8,128)S(1)}, f32[240,128]{1,0:T(8,128)S(1)}, u32[]{:S(2)}, u32[]{:S(2)}) collective-permute-start(f32[240,128]{1,0:T(8,128)S(1)} %add.160.a_ref), channel_id=1, source_target_pairs={{0,24},{4,28},{8,16},{12,20},{16,8},{20,12},{24,0},{28,4},{1,25},{... | collective-permute-start | bytes 368648 | tf_op jit(solution)/shard_map/ppermute | solution.py:347
  35.9 0.0 collective-permute-done.8
  35.9 1.9 %collective-permute-start.9 = (f32[240,128]{1,0:T(8,128)S(1)}, f32[240,128]{1,0:T(8,128)S(1)}, u32[]{:S(2)}, u32[]{:S(2)}) collective-permute-start(f32[240,128]{1,0:T(8,128)S(1)} %add.170.b_ref), channel_id=1, source_target_pairs={{0,8},{4,12},{8,0},{12,4},{16,24},{20,28},{24,16},{28,20},{1,9},{5... | collective-permute-start | bytes 368648 | tf_op jit(solution)/shard_map/ppermute | solution.py:347
  37.9 1.3 %collective-permute-done.4.got_a_ref = f32[240,128]{1,0:T(8,128)S(1)} collective-permute-done((f32[240,128]{1,0:T(8,128)S(1)}, f32[240,128]{1,0:T(8,128)S(1)}, u32[]{:S(2)}, u32[]{:S(2)}) %collective-permute-start.4) | collective-permute-done | bytes 122912 | tf_op jit(solution)/shard_map/ppermute | solution.py:347
  39.2 1.7 %collective-permute-done.9.got_b_ref = f32[240,128]{1,0:T(8,128)S(1)} collective-permute-done((f32[240,128]{1,0:T(8,128)S(1)}, f32[240,128]{1,0:T(8,128)S(1)}, u32[]{:S(2)}, u32[]{:S(2)}) %collective-permute-start.9) | collective-permute-done | bytes 122912 | tf_op jit(solution)/shard_map/ppermute | solution.py:347
  40.9 0.6 shard_map.39
  41.5 0.1 collective-permute-start.10
  41.6 0.5 collective-permute-start.13
  42.1 0.8 %collective-permute-done.10 = f32[192,128]{1,0:T(8,128)S(1)} collective-permute-done((f32[192,128]{1,0:T(8,128)S(1)}, f32[192,128]{1,0:T(8,128)S(1)}, u32[]{:S(2)}, u32[]{:S(2)}) %collective-permute-start.10) | collective-permute-done | bytes 98336 | tf_op jit(solution)/shard_map/ppermute | solution.py:347
  42.9 1.6 %collective-permute-start.11 = (f32[240,128]{1,0:T(8,128)S(1)}, f32[240,128]{1,0:T(8,128)S(1)}, u32[]{:S(2)}, u32[]{:S(2)}) collective-permute-start(f32[240,128]{1,0:T(8,128)S(1)} %pad_maximum_fusion.3), channel_id=1, source_target_pairs={{0,2},{1,3},{2,0},{3,1},{4,6},{5,7},{6,4},{7,5},{8,10},{9,11},{10,... | collective-permute-start | bytes 368648 | tf_op jit(solution)/shard_map/ppermute | solution.py:347
  44.5 0.0 collective-permute-done.13
  44.5 1.6 %collective-permute-start.14 = (f32[240,128]{1,0:T(8,128)S(1)}, f32[240,128]{1,0:T(8,128)S(1)}, u32[]{:S(2)}, u32[]{:S(2)}) collective-permute-start(f32[240,128]{1,0:T(8,128)S(1)} %pad_maximum_fusion.4), channel_id=1, source_target_pairs={{0,4},{4,0},{8,12},{12,8},{16,20},{20,16},{24,28},{28,24},{1,5},{5... | collective-permute-start | bytes 368648 | tf_op jit(solution)/shard_map/ppermute | solution.py:347
  46.1 2.3 %collective-permute-done.11 = f32[240,128]{1,0:T(8,128)S(1)} collective-permute-done((f32[240,128]{1,0:T(8,128)S(1)}, f32[240,128]{1,0:T(8,128)S(1)}, u32[]{:S(2)}, u32[]{:S(2)}) %collective-permute-start.11) | collective-permute-done | bytes 122912 | tf_op jit(solution)/shard_map/ppermute | solution.py:347
  48.4 1.6 %collective-permute-start.12 = (f32[288,128]{1,0:T(8,128)S(1)}, f32[288,128]{1,0:T(8,128)S(1)}, u32[]{:S(2)}, u32[]{:S(2)}) collective-permute-start(f32[288,128]{1,0:T(8,128)S(1)} %pad_maximum_fusion.1), channel_id=1, source_target_pairs={{0,4},{4,0},{8,12},{12,8},{16,20},{20,16},{24,28},{28,24},{1,5},{5... | collective-permute-start | bytes 442376 | tf_op jit(solution)/shard_map/ppermute | solution.py:347
  50.0 0.0 collective-permute-done.14
  50.1 1.6 %collective-permute-start.15 = (f32[288,128]{1,0:T(8,128)S(1)}, f32[288,128]{1,0:T(8,128)S(1)}, u32[]{:S(2)}, u32[]{:S(2)}) collective-permute-start(f32[288,128]{1,0:T(8,128)S(1)} %pad_maximum_fusion.2), channel_id=1, source_target_pairs={{0,2},{1,3},{2,0},{3,1},{4,6},{5,7},{6,4},{7,5},{8,10},{9,11},{10,... | collective-permute-start | bytes 442376 | tf_op jit(solution)/shard_map/ppermute | solution.py:347
  51.6 2.0 %collective-permute-done.12 = f32[288,128]{1,0:T(8,128)S(1)} collective-permute-done((f32[288,128]{1,0:T(8,128)S(1)}, f32[288,128]{1,0:T(8,128)S(1)}, u32[]{:S(2)}, u32[]{:S(2)}) %collective-permute-start.12) | collective-permute-done | bytes 147488 | tf_op jit(solution)/shard_map/ppermute | solution.py:347
  53.7 1.6 %collective-permute-done.15 = f32[288,128]{1,0:T(8,128)S(1)} collective-permute-done((f32[288,128]{1,0:T(8,128)S(1)}, f32[288,128]{1,0:T(8,128)S(1)}, u32[]{:S(2)}, u32[]{:S(2)}) %collective-permute-start.15) | collective-permute-done | bytes 147488 | tf_op jit(solution)/shard_map/ppermute | solution.py:347
  55.4 0.1 collective-permute-start.16
  55.5 1.7 %collective-permute-done.16.refs_2_ = f32[2,384,128]{2,1,0:T(8,128)S(1)} collective-permute-done((f32[2,384,128]{2,1,0:T(8,128)S(1)}, f32[2,384,128]{2,1,0:T(8,128)S(1)}, u32[]{:S(2)}, u32[]{:S(2)}) %collective-permute-start.16) | collective-permute-done | bytes 393248 | tf_op jit(solution)/shard_map/ppermute | solution.py:347
  57.2 17.2 %shard_map.40 = f32[2048,384]{1,0:T(8,128)} custom-call(s32[1]{0:T(128)} %bitcast.core_ref.refs_0_, f32[2,384,128]{2,1,0:T(8,128)S(1)} %pad_maximum_fusion.refs_1_, f32[2,384,128]{2,1,0:T(8,128)S(1)} %collective-permute-done.16.refs_2_, f32[2048,256]{1,0:T(8,128)} %refs_3_.1, f32[2048,128]{1,0:T(8,128)} %refs_4_.1), custom_call_target="tpu_custom_call" | custom-call | tf_op jit(solution)/shard_map/pallas_call | solution.py:322
  (30 shorter events, 0.5 us)
Async XLA Ops:
  6.3 5.2 %collective-permute-start = (f32[4,240,128]{2,1,0:T(8,128)S(1)}, f32[4,240,128]{2,1,0:T(8,128)S(1)}, u32[]{:S(2)}, u32[]{:S(2)}) collective-permute-start(f32[4,240,128]{2,1,0:T(8,128)S(1)} %get-tuple-element.18), channel_id=1, source_target_pairs={{0,1},{1,0},{2,3},{3,2},{4,5},{5,4},{6,7},{7,6},{8,9},{9,8},{10,11... | collective-permute-start | bytes 1474568 | tf_op jit(solution)/shard_map/ppermute | solution.py:347
  6.9 7.7 %collective-permute-start.5 = (f32[4,240,128]{2,1,0:T(8,128)S(1)}, f32[4,240,128]{2,1,0:T(8,128)S(1)}, u32[]{:S(2)}, u32[]{:S(2)}) collective-permute-start(f32[4,240,128]{2,1,0:T(8,128)S(1)} %get-tuple-element.20), channel_id=1, source_target_pairs={{0,1},{1,0},{2,3},{3,2},{4,5},{5,4},{6,7},{7,6},{8,9},{9,8},{10,11... | collective-permute-start | bytes 1474568 | tf_op jit(solution)/shard_map/ppermute | solution.py:347
  11.5 9.2 %collective-permute-start.1 = (f32[2,240,128]{2,1,0:T(8,128)S(1)}, f32[2,240,128]{2,1,0:T(8,128)S(1)}, u32[]{:S(2)}, u32[]{:S(2)}) collective-permute-start(f32[2,240,128]{2,1,0:T(8,128)S(1)} %add_bitcast_fusion.1), channel_id=1, source_target_pairs={{0,2},{1,3},{2,0},{3,1},{4,6},{5,7},{6,4},{7,5},{8,10},{9,11},{10,... | collective-permute-start | bytes 737288 | tf_op jit(solution)/shard_map/ppermute | solution.py:347
  14.6 8.0 %collective-permute-start.6 = (f32[2,240,128]{2,1,0:T(8,128)S(1)}, f32[2,240,128]{2,1,0:T(8,128)S(1)}, u32[]{:S(2)}, u32[]{:S(2)}) collective-permute-start(f32[2,240,128]{2,1,0:T(8,128)S(1)} %add_bitcast_fusion), channel_id=1, source_target_pairs={{0,4},{4,0},{8,12},{12,8},{16,20},{20,16},{24,28},{28,24},{1,5},{5... | collective-permute-start | bytes 737288 | tf_op jit(solution)/shard_map/ppermute | solution.py:347
  20.8 4.9 %collective-permute-start.2 = (f32[240,128]{1,0:T(8,128)S(1)}, f32[240,128]{1,0:T(8,128)S(1)}, u32[]{:S(2)}, u32[]{:S(2)}) collective-permute-start(f32[240,128]{1,0:T(8,128)S(1)} %bitcast_add_fusion.2), channel_id=1, source_target_pairs={{0,4},{4,0},{8,12},{12,8},{16,20},{20,16},{24,28},{28,24},{1,5},{5... | collective-permute-start | bytes 368648 | tf_op jit(solution)/shard_map/ppermute | solution.py:347
  22.6 5.0 %collective-permute-start.7 = (f32[240,128]{1,0:T(8,128)S(1)}, f32[240,128]{1,0:T(8,128)S(1)}, u32[]{:S(2)}, u32[]{:S(2)}) collective-permute-start(f32[240,128]{1,0:T(8,128)S(1)} %bitcast_add_fusion), channel_id=1, source_target_pairs={{0,2},{1,3},{2,0},{3,1},{4,6},{5,7},{6,4},{7,5},{8,10},{9,11},{10,... | collective-permute-start | bytes 368648 | tf_op jit(solution)/shard_map/ppermute | solution.py:347
  25.7 6.3 %collective-permute-start.3 = (f32[240,128]{1,0:T(8,128)S(1)}, f32[240,128]{1,0:T(8,128)S(1)}, u32[]{:S(2)}, u32[]{:S(2)}) collective-permute-start(f32[240,128]{1,0:T(8,128)S(1)} %fusion.1), channel_id=1, source_target_pairs={{0,8},{4,12},{8,0},{12,4},{16,24},{20,28},{24,16},{28,20},{1,9},{5... | collective-permute-start | bytes 368648 | tf_op jit(solution)/shard_map/ppermute | solution.py:347
  27.6 8.3 %collective-permute-start.8 = (f32[240,128]{1,0:T(8,128)S(1)}, f32[240,128]{1,0:T(8,128)S(1)}, u32[]{:S(2)}, u32[]{:S(2)}) collective-permute-start(f32[240,128]{1,0:T(8,128)S(1)} %fusion), channel_id=1, source_target_pairs={{0,24},{4,28},{8,16},{12,20},{16,8},{20,12},{24,0},{28,4},{1,25},{... | collective-permute-start | bytes 368648 | tf_op jit(solution)/shard_map/ppermute | solution.py:347
  32.0 7.2 %collective-permute-start.4 = (f32[240,128]{1,0:T(8,128)S(1)}, f32[240,128]{1,0:T(8,128)S(1)}, u32[]{:S(2)}, u32[]{:S(2)}) collective-permute-start(f32[240,128]{1,0:T(8,128)S(1)} %add.160.a_ref), channel_id=1, source_target_pairs={{0,24},{4,28},{8,16},{12,20},{16,8},{20,12},{24,0},{28,4},{1,25},{... | collective-permute-start | bytes 368648 | tf_op jit(solution)/shard_map/ppermute | solution.py:347
  35.9 4.9 %collective-permute-start.9 = (f32[240,128]{1,0:T(8,128)S(1)}, f32[240,128]{1,0:T(8,128)S(1)}, u32[]{:S(2)}, u32[]{:S(2)}) collective-permute-start(f32[240,128]{1,0:T(8,128)S(1)} %add.170.b_ref), channel_id=1, source_target_pairs={{0,8},{4,12},{8,0},{12,4},{16,24},{20,28},{24,16},{28,20},{1,9},{5... | collective-permute-start | bytes 368648 | tf_op jit(solution)/shard_map/ppermute | solution.py:347
  41.5 1.4 %collective-permute-start.10 = (f32[192,128]{1,0:T(8,128)S(1)}, f32[192,128]{1,0:T(8,128)S(1)}, u32[]{:S(2)}, u32[]{:S(2)}) collective-permute-start(f32[192,128]{1,0:T(8,128)S(1)} %get-tuple-element.22), channel_id=1, source_target_pairs={{0,1},{1,0},{2,3},{3,2},{4,5},{5,4},{6,7},{7,6},{8,9},{9,8},{10,11... | collective-permute-start | bytes 294920 | tf_op jit(solution)/shard_map/ppermute | solution.py:347
  41.6 2.9 %collective-permute-start.13 = (f32[192,128]{1,0:T(8,128)S(1)}, f32[192,128]{1,0:T(8,128)S(1)}, u32[]{:S(2)}, u32[]{:S(2)}) collective-permute-start(f32[192,128]{1,0:T(8,128)S(1)} %get-tuple-element.25), channel_id=1, source_target_pairs={{0,1},{1,0},{2,3},{3,2},{4,5},{5,4},{6,7},{7,6},{8,9},{9,8},{10,11... | collective-permute-start | bytes 294920 | tf_op jit(solution)/shard_map/ppermute | solution.py:347
  42.9 5.4 %collective-permute-start.11 = (f32[240,128]{1,0:T(8,128)S(1)}, f32[240,128]{1,0:T(8,128)S(1)}, u32[]{:S(2)}, u32[]{:S(2)}) collective-permute-start(f32[240,128]{1,0:T(8,128)S(1)} %pad_maximum_fusion.3), channel_id=1, source_target_pairs={{0,2},{1,3},{2,0},{3,1},{4,6},{5,7},{6,4},{7,5},{8,10},{9,11},{10,... | collective-permute-start | bytes 368648 | tf_op jit(solution)/shard_map/ppermute | solution.py:347
  44.5 5.5 %collective-permute-start.14 = (f32[240,128]{1,0:T(8,128)S(1)}, f32[240,128]{1,0:T(8,128)S(1)}, u32[]{:S(2)}, u32[]{:S(2)}) collective-permute-start(f32[240,128]{1,0:T(8,128)S(1)} %pad_maximum_fusion.4), channel_id=1, source_target_pairs={{0,4},{4,0},{8,12},{12,8},{16,20},{20,16},{24,28},{28,24},{1,5},{5... | collective-permute-start | bytes 368648 | tf_op jit(solution)/shard_map/ppermute | solution.py:347
  48.4 5.2 %collective-permute-start.12 = (f32[288,128]{1,0:T(8,128)S(1)}, f32[288,128]{1,0:T(8,128)S(1)}, u32[]{:S(2)}, u32[]{:S(2)}) collective-permute-start(f32[288,128]{1,0:T(8,128)S(1)} %pad_maximum_fusion.1), channel_id=1, source_target_pairs={{0,4},{4,0},{8,12},{12,8},{16,20},{20,16},{24,28},{28,24},{1,5},{5... | collective-permute-start | bytes 442376 | tf_op jit(solution)/shard_map/ppermute | solution.py:347
  50.1 5.2 %collective-permute-start.15 = (f32[288,128]{1,0:T(8,128)S(1)}, f32[288,128]{1,0:T(8,128)S(1)}, u32[]{:S(2)}, u32[]{:S(2)}) collective-permute-start(f32[288,128]{1,0:T(8,128)S(1)} %pad_maximum_fusion.2), channel_id=1, source_target_pairs={{0,2},{1,3},{2,0},{3,1},{4,6},{5,7},{6,4},{7,5},{8,10},{9,11},{10,... | collective-permute-start | bytes 442376 | tf_op jit(solution)/shard_map/ppermute | solution.py:347
  55.4 1.8 %collective-permute-start.16 = (f32[2,384,128]{2,1,0:T(8,128)S(1)}, f32[2,384,128]{2,1,0:T(8,128)S(1)}, u32[]{:S(2)}, u32[]{:S(2)}) collective-permute-start(f32[2,384,128]{2,1,0:T(8,128)S(1)} %pad_maximum_fusion.refs_1_), channel_id=1, source_target_pairs={{0,1},{1,0},{2,3},{3,2},{4,5},{5,4},{6,7},{7,6},{8,9},{9,8},{10,11... | collective-permute-start | bytes 1179656 | tf_op jit(solution)/shard_map/ppermute | solution.py:347

commit v2 on v1

--- a/solution.py
+++ b/solution.py
@@ -11,6 +11,7 @@
 BF16 = jnp.bfloat16
 LANES = 128
 BLOCK = 16
+PANEL = 2
 CHUNKS = 4
 LIMIT = pltpu.CompilerParams(vmem_limit_bytes=32 << 20)
 VMEM = pltpu.VMEM
@@ -143,67 +144,84 @@
     return call(False, own), theirs
 
 
-def factor(m_ref):
+def eliminate(parts, tile, first):
+    height = parts[0].shape[0]
+    row = lax.broadcasted_iota(jnp.int32, (height, LANES), 0)
+    lane = lax.broadcasted_iota(jnp.int32, (height, LANES), 1) - first
+    cols = [
+        jnp.take_along_axis(parts[tile], jnp.full((height, LANES), first + q, jnp.int32), axis=1) for q in range(BLOCK)
+    ]
+    parts = list(parts)
+    parts[tile] = jnp.where((lane >= 0) & (lane < BLOCK), jnp.where(lane == row, 1.0, 0.0), parts[tile])
+    head = row[:BLOCK]
+    pivots = jnp.ones((BLOCK, LANES), F32)
+
+    def spot(value, index, tall):
+        return jnp.broadcast_to(value[index : index + 1, :], (tall, LANES))
+
+    for p in range(0, BLOCK, 2):
+        low = (p + 1) // 8 * 8
+        a, b, c = spot(cols[p], p, height), spot(cols[p], p + 1, height), spot(cols[p + 1], p + 1, height)
+        det = a * c - b * b
+        over_det, over_a = 1.0 / det, 1.0 / a
+        pivots = jnp.where(head == p, a[:BLOCK], jnp.where(head == p + 1, (det * over_a)[:BLOCK], pivots))
+        under = row[low:] > p + 1
+        x, y = cols[p][low:], cols[p + 1][low:]
+        a, b, c, ratio, over_det = (v[low:] for v in (a, b, c, b * over_a, over_det))
+        mult = jnp.where(under, (x * c - y * b) * over_det, 0.0)
+        next_mult = jnp.where(under, (y * a - x * b) * over_det, 0.0)
+
+        def cleared(value, first_mult, p=p, low=low, next_mult=next_mult):
+            tall = height - low
+            new = value[low:] - first_mult * spot(value, p, tall) - next_mult * spot(value, p + 1, tall)
+            return jnp.concatenate([value[:low], new], axis=0) if low else new
+
+        for q in range(p + 2, BLOCK):
+            cols[q] = cleared(cols[q], mult)
+        mult = jnp.where(row[low:] == p + 1, ratio, mult)
+        parts = [cleared(value, mult) for value in parts]
+    inv = lax.rsqrt(pivots)
+    return [value[:BLOCK] * inv for value in parts], [value[BLOCK:] for value in parts]
+
+
+def factor(m_ref, ready, beside):
     n = m_ref.shape[0]
     tiles = n // LANES
+    panel = BLOCK * PANEL
     for phase in range(tiles):
         base = LANES * phase
-
-        def step(k, carry, base=base):
-            start = base + k * BLOCK
-            mine = pl.ds(pl.multiple_of(start, BLOCK), BLOCK)
+        last = phase == tiles - 1
+        if last:
+            ready()
+
+        def step(k, carry, base=base, phase=phase, last=last):
+            start = base + k * panel
+            if last:
+                beside(k)
+            mine = pl.ds(pl.multiple_of(start, panel), panel)
             rows = m_ref[mine, :]
-            diag = rows[:, base : base + LANES]
-            row = lax.broadcasted_iota(jnp.int32, (BLOCK, LANES), 0)
-            cols = [
-                jnp.take_along_axis(diag, jnp.full((BLOCK, LANES), k * BLOCK + q, jnp.int32), axis=1)
-                for q in range(BLOCK)
-            ]
-            lane = lax.broadcasted_iota(jnp.int32, (BLOCK, n), 1) - start
-            sub = lax.broadcasted_iota(jnp.int32, (BLOCK, n), 0)
-            unit = jnp.where(lane == sub, 1.0, 0.0)
-            work = jnp.where((lane >= 0) & (lane < BLOCK), unit, rows)
-            parts = [work[:, t * LANES : (t + 1) * LANES] for t in range(tiles)]
-            pivots = jnp.ones((BLOCK, LANES), F32)
-            for p in range(0, BLOCK, 2):
-                base_row = (p + 1) // 8 * 8
-
-                def wide_row(value, index, low=base_row):
-                    return jnp.broadcast_to(value[index : index + 1, :], (BLOCK - low, LANES))
-
-                a, b, c = wide_row(cols[p], p, 0), wide_row(cols[p], p + 1, 0), wide_row(cols[p + 1], p + 1, 0)
-                det = a * c - b * b
-                over_det, over_a = 1.0 / det, 1.0 / a
-                pivots = jnp.where(row == p, a, jnp.where(row == p + 1, det * over_a, pivots))
-                under = row[base_row:] > p + 1
-                x, y = cols[p][base_row:], cols[p + 1][base_row:]
-                a, b, c, ratio, over_det = (v[base_row:] for v in (a, b, c, b * over_a, over_det))
-                mult = jnp.where(under, (x * c - y * b) * over_det, 0.0)
-                next_mult = jnp.where(under, (y * a - x * b) * over_det, 0.0)
-
-                def cleared(value, first_mult, p=p, low=base_row, next_mult=next_mult, wide_row=wide_row):
-                    new = value[low:] - first_mult * wide_row(value, p) - next_mult * wide_row(value, p + 1)
-                    return jnp.concatenate([value[:low], new], axis=0) if low else new
-
-                for q in range(p + 2, BLOCK):
-                    cols[q] = cleared(cols[q], mult)
-                mult = jnp.where(row[base_row:] == p + 1, ratio, mult)
-                parts = [cleared(value, mult) for value in parts]
-            inv = lax.rsqrt(pivots)
-            done = jnp.concatenate([x * inv for x in parts], axis=1)
-            rest = jnp.where(lane >= BLOCK, done, 0.0)[:, base:]
+            parts = [rows[:, t * LANES : (t + 1) * LANES] for t in range(tiles)]
+            blocks = []
+            for b in range(PANEL):
+                top, parts = eliminate(parts, phase, k * panel + b * BLOCK)
+                blocks.append(jnp.concatenate(top, axis=1))
+            done = jnp.concatenate(blocks, axis=0)
+            lane = lax.broadcasted_iota(jnp.int32, (panel, n), 1) - start
+            sub = lax.broadcasted_iota(jnp.int32, (panel, n), 0)
+            rest = jnp.where(lane >= panel, done, 0.0)[:, base:]
+            done = jnp.where((lane < panel) & (lane > sub), 0.0, done)
             h, m, l = thirds(done)
             hr, mr, lr = thirds(rest)
-            right = jnp.concatenate([h, m, h, l, h, m, l, m], axis=0)
-            left = jnp.concatenate([hr, hr, mr, hr, lr, mr, mr, lr], axis=0)
+            right = jnp.concatenate([h, m, h, l, h, m], axis=0)
+            left = jnp.concatenate([hr, hr, mr, hr, lr, mr], axis=0)
             update = contract(left, right, 0, 0)
             lanes = lax.broadcasted_iota(jnp.int32, (n - base, n), 1) - start
-            keep = (lanes < 0) | (lanes >= BLOCK)
+            keep = (lanes < 0) | (lanes >= panel)
             m_ref[base:, :] = jnp.where(keep, m_ref[base:, :], 0.0) - update
             m_ref[mine, :] = done
             return carry
 
-        lax.fori_loop(0, LANES // BLOCK, step, 0)
+        lax.fori_loop(0, LANES // panel, step, 0)
 
 
 def hess_kernel(core_ref, a_ref, got_a_ref, b_ref, got_b_ref, keep_a_ref, keep_b_ref, give_a_ref, give_b_ref, gram_a_ref, gram_b_ref):
@@ -239,7 +257,7 @@
     )(core, a, got_a, b, got_b)
 
 
-def whiten_kernel(scale, lead_ref, own_ref, got_ref, basis_ref, new_ref, out_ref, m_ref, vec_ref, res_ref, sems):
+def whiten_kernel(scale, lead_ref, own_ref, got_ref, basis_ref, new_ref, out_ref, m_ref, vec_ref, res_ref, mix_ref, sems):
     n = m_ref.shape[0]
     rows, width = basis_ref.shape
     chunk = rows // CHUNKS
@@ -277,37 +295,48 @@
     s_vv, s_vw, s_ww = full[:width, :width], full[:width, width:], full[width:, width:]
     second = s_vw - exact(s_vv, s_vw, 1, 0)
     summed = s_vw + second
-    gram = s_ww - exact(summed, s_vw, 0, 0) - exact(s_vw, summed, 0, 0)
-    gram = gram + exact(summed, exact(s_vv, summed, 1, 0), 0, 0)
-    corner = exact(summed, summed, 0, 0) + gram
+    moved = second + exact(s_vv, summed, 1, 0)
+    corner = s_ww + exact(
+        jnp.concatenate([summed, s_vw], axis=0), jnp.concatenate([moved, -summed], axis=0), 0, 0
+    )
     r = lax.broadcasted_iota(jnp.int32, (width, width), 0)
     c = lax.broadcasted_iota(jnp.int32, (width, width), 1)
     m_ref[:width, :width] = hess[:width, :width] + jnp.where(r == c, 1.0, 0.0)
     m_ref[:width, width:] = hess[:width, width:] + summed
     m_ref[width:, :width] = hess[width:, :width] + summed.T
     m_ref[width:, width:] = hess[width:, width:] + corner
-    factor(m_ref)
-    r = lax.broadcasted_iota(jnp.int32, (n, n), 0)
-    c = lax.broadcasted_iota(jnp.int32, (n, n), 1)
-    mix = halves(jnp.where(r >= c, m_ref[...], 0.0).T)
-    corner = tuple(x[:width, :width] for x in mix)
-    last = tuple(x[:, width:] for x in mix)
-
-    def store(k):
-        at = pl.ds(k * chunk, chunk)
-        return pltpu.make_async_copy(res_ref.at[at, :], out_ref.at[at, :], sems.at[k, 2])
-
+    lead_cols = n - LANES
+
+    def store(k, late):
+        at = pl.ds(pl.multiple_of(k * chunk, chunk), chunk)
+        lanes = pl.ds(lead_cols, LANES) if late else pl.ds(0, lead_cols)
+        return pltpu.make_async_copy(res_ref.at[at, lanes], out_ref.at[at, lanes], sems.at[k, 2 + late])
+
+    def triangle(low, high):
+        r = lax.broadcasted_iota(jnp.int32, (high - low, high), 0) + low
+        c = lax.broadcasted_iota(jnp.int32, (high - low, high), 1)
+        return halves(jnp.where(r >= c, m_ref[low:high, :high], 0.0).T)
+
+    def ready():
+        mix_ref[0], mix_ref[1] = triangle(0, lead_cols)
+        for k in range(CHUNKS):
+            for copy in loads(k):
+                copy.wait()
+
+    def beside(k):
+        at = pl.ds(pl.multiple_of(k * chunk, chunk), chunk)
+        res_ref[at, :lead_cols] = three(halves(vec_ref[at, :lead_cols]), (mix_ref[0], mix_ref[1]), 1, 0)
+        store(k, 0).start()
+
+    factor(m_ref, ready, beside)
+    last = triangle(lead_cols, n)
     for k in range(CHUNKS):
         at = slice(k * chunk, (k + 1) * chunk)
-        for copy in loads(k):
-            copy.wait()
-        value = halves(vec_ref[at, :])
-        old = tuple(x[:, :width] for x in value)
-        res_ref[at, :width] = three(old, corner, 1, 0)
-        res_ref[at, width:] = three(value, last, 1, 0)
-        store(k).start()
+        res_ref[at, lead_cols:] = three(halves(vec_ref[at, :]), last, 1, 0)
+        store(k, 1).start()
     for k in range(CHUNKS):
-        store(k).wait()
+        store(k, 0).wait()
+        store(k, 1).wait()
 
 
 def whiten(scale, lead, own, got, basis, new_vectors):
@@ -328,7 +357,8 @@
             VMEM((n, n), F32),
             VMEM((rows, n), F32),
             VMEM((rows, n), F32),
-            pltpu.SemaphoreType.DMA((CHUNKS, 3)),
+            VMEM((2, n - LANES, n - LANES), BF16),
+            pltpu.SemaphoreType.DMA((CHUNKS, 4)),
         ],
         compiler_params=LIMIT,
     )(lead, own, got, basis, new_vectors)

time: 74.7 us -> 71.1 us (0.952)
  Pallas kernels: 28.6 us -> 25 us
    pallas_call x1, Pallas kernels: 17.2 us -> 13.6 us  [whiten(): pl.pallas_call(kernel, in_specs=[pl.BlockSpec(memory_space=pltpu.SMEM), i...]
  transfers between devices with their start and end apart: 17 -> 17, of which waited for: 10 -> 10; matrix products, arithmetic and copies ran while one was open for 0% -> 1% of each run, Pallas kernels for 6% -> 6%
where the time goes in v2:
time: 71.1 us; the launch traced here: 70.9 us
  starting transfers between devices  26.7 us (38%)
  Pallas kernels  25 us (35%)
  waiting for transfers between devices  18.3 us (26%)
    ppermute x17, starting transfers between devices, swap(): return lax.ppermute(value, axis, [(i, i ^ mask) for i in range(size)])  26.7 us
    ppermute x17, waiting for transfers between devices, swap(): return lax.ppermute(value, axis, [(i, i ^ mask) for i in range(size)])  18.3 us
    pallas_call x1, Pallas kernels, whiten(): pl.pallas_call(kernel, in_specs=[pl.BlockSpec(memory_space=pltpu.SMEM), i...  13.6 us
    pallas_call x2, Pallas kernels, call(): pl.pallas_call(functools.partial(products_kernel, first), in_specs=[scala...  10.8 us
  transfers between devices with their start and end apart: 17, of which 10 were waited for; matrix products, arithmetic and copies ran while one was open for 1% of the time, Pallas kernels for 6%

profile of v2, /device:TPU:0, one launch (start us, length us, event | category | flops | bytes accessed | tf_op | source)
XLA Modules:
  0.0 70.9 jit_solution(11814994927620317404)
XLA Ops:
  0.0 6.3 %shard_map.37 = (f32[4,240,128]{2,1,0:T(8,128)S(1)}, f32[4,240,128]{2,1,0:T(8,128)S(1)}, f32[384,128]{1,0:T(8,128)S(1)}) custom-call(s32[1]{0:T(128)} %bitcast.core_ref.refs_0_, f32[2048,256]{1,0:T(8,128)} %refs_3_.1, f32[2048,128]{1,0:T(8,128)} %refs_4_.1, f32[2048,1024]{1,0:T(8,128)} %jac_ref.3), custom_call_target="tpu_custom_call" | custom-call | tf_op jit(solution)/shard_map/pallas_call | solution.py:130
  6.3 0.6 collective-permute-start
  6.9 0.1 collective-permute-start.5
  7.0 4.5 %shard_map.38 = (f32[4,240,128]{2,1,0:T(8,128)S(1)}, f32[4,240,128]{2,1,0:T(8,128)S(1)}) custom-call(s32[1]{0:T(128)} %bitcast.core_ref.refs_0_, f32[2048,256]{1,0:T(8,128)} %refs_3_.1, f32[2048,128]{1,0:T(8,128)} %refs_4_.1, f32[2048,1024]{1,0:T(8,128)} %jac_ref.3, f32[384,128]{1,0:T(8,128)S(1)} %get-tuple-element.16.refs_0_), custom_call_target="tpu_custom_call" | custom-call | tf_op jit(solution)/shard_map/pallas_call | solution.py:130
  11.5 0.0 collective-permute-done
  11.5 3.0 %collective-permute-start.1 = (f32[2,240,128]{2,1,0:T(8,128)S(1)}, f32[2,240,128]{2,1,0:T(8,128)S(1)}, u32[]{:S(2)}, u32[]{:S(2)}) collective-permute-start(f32[2,240,128]{2,1,0:T(8,128)S(1)} %add_bitcast_fusion.1), channel_id=1, source_target_pairs={{0,2},{1,3},{2,0},{3,1},{4,6},{5,7},{6,4},{7,5},{8,10},{9,11},{10,... | collective-permute-start | bytes 737288 | tf_op jit(solution)/shard_map/ppermute | solution.py:377
  14.5 0.0 collective-permute-done.5
  14.6 1.6 %collective-permute-start.6 = (f32[2,240,128]{2,1,0:T(8,128)S(1)}, f32[2,240,128]{2,1,0:T(8,128)S(1)}, u32[]{:S(2)}, u32[]{:S(2)}) collective-permute-start(f32[2,240,128]{2,1,0:T(8,128)S(1)} %add_bitcast_fusion), channel_id=1, source_target_pairs={{0,4},{4,0},{8,12},{12,8},{16,20},{20,16},{24,28},{28,24},{1,5},{5... | collective-permute-start | bytes 737288 | tf_op jit(solution)/shard_map/ppermute | solution.py:377
  16.1 4.6 %collective-permute-done.1 = f32[2,240,128]{2,1,0:T(8,128)S(1)} collective-permute-done((f32[2,240,128]{2,1,0:T(8,128)S(1)}, f32[2,240,128]{2,1,0:T(8,128)S(1)}, u32[]{:S(2)}, u32[]{:S(2)}) %collective-permute-start.1) | collective-permute-done | bytes 245792 | tf_op jit(solution)/shard_map/ppermute | solution.py:377
  20.8 1.8 %collective-permute-start.2 = (f32[240,128]{1,0:T(8,128)S(1)}, f32[240,128]{1,0:T(8,128)S(1)}, u32[]{:S(2)}, u32[]{:S(2)}) collective-permute-start(f32[240,128]{1,0:T(8,128)S(1)} %bitcast_add_fusion.2), channel_id=1, source_target_pairs={{0,4},{4,0},{8,12},{12,8},{16,20},{20,16},{24,28},{28,24},{1,5},{5... | collective-permute-start | bytes 368648 | tf_op jit(solution)/shard_map/ppermute | solution.py:377
  22.5 0.0 collective-permute-done.6
  22.6 1.6 %collective-permute-start.7 = (f32[240,128]{1,0:T(8,128)S(1)}, f32[240,128]{1,0:T(8,128)S(1)}, u32[]{:S(2)}, u32[]{:S(2)}) collective-permute-start(f32[240,128]{1,0:T(8,128)S(1)} %bitcast_add_fusion), channel_id=1, source_target_pairs={{0,2},{1,3},{2,0},{3,1},{4,6},{5,7},{6,4},{7,5},{8,10},{9,11},{10,... | collective-permute-start | bytes 368648 | tf_op jit(solution)/shard_map/ppermute | solution.py:377
  24.1 1.6 %collective-permute-done.2 = f32[240,128]{1,0:T(8,128)S(1)} collective-permute-done((f32[240,128]{1,0:T(8,128)S(1)}, f32[240,128]{1,0:T(8,128)S(1)}, u32[]{:S(2)}, u32[]{:S(2)}) %collective-permute-start.2) | collective-permute-done | bytes 122912 | tf_op jit(solution)/shard_map/ppermute | solution.py:377
  25.7 1.9 %collective-permute-start.3 = (f32[240,128]{1,0:T(8,128)S(1)}, f32[240,128]{1,0:T(8,128)S(1)}, u32[]{:S(2)}, u32[]{:S(2)}) collective-permute-start(f32[240,128]{1,0:T(8,128)S(1)} %fusion.1), channel_id=1, source_target_pairs={{0,8},{4,12},{8,0},{12,4},{16,24},{20,28},{24,16},{28,20},{1,9},{5... | collective-permute-start | bytes 368648 | tf_op jit(solution)/shard_map/ppermute | solution.py:377
  27.6 0.0 collective-permute-done.7
  27.6 3.6 %collective-permute-start.8 = (f32[240,128]{1,0:T(8,128)S(1)}, f32[240,128]{1,0:T(8,128)S(1)}, u32[]{:S(2)}, u32[]{:S(2)}) collective-permute-start(f32[240,128]{1,0:T(8,128)S(1)} %fusion), channel_id=1, source_target_pairs={{0,24},{4,28},{8,16},{12,20},{16,8},{20,12},{24,0},{28,4},{1,25},{... | collective-permute-start | bytes 368648 | tf_op jit(solution)/shard_map/ppermute | solution.py:377
  31.2 0.8 %collective-permute-done.3 = f32[240,128]{1,0:T(8,128)S(1)} collective-permute-done((f32[240,128]{1,0:T(8,128)S(1)}, f32[240,128]{1,0:T(8,128)S(1)}, u32[]{:S(2)}, u32[]{:S(2)}) %collective-permute-start.3) | collective-permute-done | bytes 122912 | tf_op jit(solution)/shard_map/ppermute | solution.py:377
  32.0 3.9 %collective-permute-start.4 = (f32[240,128]{1,0:T(8,128)S(1)}, f32[240,128]{1,0:T(8,128)S(1)}, u32[]{:S(2)}, u32[]{:S(2)}) collective-permute-start(f32[240,128]{1,0:T(8,128)S(1)} %add.160.a_ref), channel_id=1, source_target_pairs={{0,24},{4,28},{8,16},{12,20},{16,8},{20,12},{24,0},{28,4},{1,25},{... | collective-permute-start | bytes 368648 | tf_op jit(solution)/shard_map/ppermute | solution.py:377
  35.9 0.0 collective-permute-done.8
  35.9 1.9 %collective-permute-start.9 = (f32[240,128]{1,0:T(8,128)S(1)}, f32[240,128]{1,0:T(8,128)S(1)}, u32[]{:S(2)}, u32[]{:S(2)}) collective-permute-start(f32[240,128]{1,0:T(8,128)S(1)} %add.170.b_ref), channel_id=1, source_target_pairs={{0,8},{4,12},{8,0},{12,4},{16,24},{20,28},{24,16},{28,20},{1,9},{5... | collective-permute-start | bytes 368648 | tf_op jit(solution)/shard_map/ppermute | solution.py:377
  37.9 1.3 %collective-permute-done.4.got_a_ref = f32[240,128]{1,0:T(8,128)S(1)} collective-permute-done((f32[240,128]{1,0:T(8,128)S(1)}, f32[240,128]{1,0:T(8,128)S(1)}, u32[]{:S(2)}, u32[]{:S(2)}) %collective-permute-start.4) | collective-permute-done | bytes 122912 | tf_op jit(solution)/shard_map/ppermute | solution.py:377
  39.2 1.7 %collective-permute-done.9.got_b_ref = f32[240,128]{1,0:T(8,128)S(1)} collective-permute-done((f32[240,128]{1,0:T(8,128)S(1)}, f32[240,128]{1,0:T(8,128)S(1)}, u32[]{:S(2)}, u32[]{:S(2)}) %collective-permute-start.9) | collective-permute-done | bytes 122912 | tf_op jit(solution)/shard_map/ppermute | solution.py:377
  40.9 0.6 shard_map.39
  41.5 0.1 collective-permute-start.10
  41.6 0.5 collective-permute-start.13
  42.1 0.8 %collective-permute-done.10 = f32[192,128]{1,0:T(8,128)S(1)} collective-permute-done((f32[192,128]{1,0:T(8,128)S(1)}, f32[192,128]{1,0:T(8,128)S(1)}, u32[]{:S(2)}, u32[]{:S(2)}) %collective-permute-start.10) | collective-permute-done | bytes 98336 | tf_op jit(solution)/shard_map/ppermute | solution.py:377
  42.9 1.6 %collective-permute-start.11 = (f32[240,128]{1,0:T(8,128)S(1)}, f32[240,128]{1,0:T(8,128)S(1)}, u32[]{:S(2)}, u32[]{:S(2)}) collective-permute-start(f32[240,128]{1,0:T(8,128)S(1)} %pad_maximum_fusion.3), channel_id=1, source_target_pairs={{0,2},{1,3},{2,0},{3,1},{4,6},{5,7},{6,4},{7,5},{8,10},{9,11},{10,... | collective-permute-start | bytes 368648 | tf_op jit(solution)/shard_map/ppermute | solution.py:377
  44.5 0.0 collective-permute-done.13
  44.5 1.6 %collective-permute-start.14 = (f32[240,128]{1,0:T(8,128)S(1)}, f32[240,128]{1,0:T(8,128)S(1)}, u32[]{:S(2)}, u32[]{:S(2)}) collective-permute-start(f32[240,128]{1,0:T(8,128)S(1)} %pad_maximum_fusion.4), channel_id=1, source_target_pairs={{0,4},{4,0},{8,12},{12,8},{16,20},{20,16},{24,28},{28,24},{1,5},{5... | collective-permute-start | bytes 368648 | tf_op jit(solution)/shard_map/ppermute | solution.py:377
  46.1 2.3 %collective-permute-done.11 = f32[240,128]{1,0:T(8,128)S(1)} collective-permute-done((f32[240,128]{1,0:T(8,128)S(1)}, f32[240,128]{1,0:T(8,128)S(1)}, u32[]{:S(2)}, u32[]{:S(2)}) %collective-permute-start.11) | collective-permute-done | bytes 122912 | tf_op jit(solution)/shard_map/ppermute | solution.py:377
  48.4 1.6 %collective-permute-start.12 = (f32[288,128]{1,0:T(8,128)S(1)}, f32[288,128]{1,0:T(8,128)S(1)}, u32[]{:S(2)}, u32[]{:S(2)}) collective-permute-start(f32[288,128]{1,0:T(8,128)S(1)} %pad_maximum_fusion.1), channel_id=1, source_target_pairs={{0,4},{4,0},{8,12},{12,8},{16,20},{20,16},{24,28},{28,24},{1,5},{5... | collective-permute-start | bytes 442376 | tf_op jit(solution)/shard_map/ppermute | solution.py:377
  50.0 0.0 collective-permute-done.14
  50.1 1.6 %collective-permute-start.15 = (f32[288,128]{1,0:T(8,128)S(1)}, f32[288,128]{1,0:T(8,128)S(1)}, u32[]{:S(2)}, u32[]{:S(2)}) collective-permute-start(f32[288,128]{1,0:T(8,128)S(1)} %pad_maximum_fusion.2), channel_id=1, source_target_pairs={{0,2},{1,3},{2,0},{3,1},{4,6},{5,7},{6,4},{7,5},{8,10},{9,11},{10,... | collective-permute-start | bytes 442376 | tf_op jit(solution)/shard_map/ppermute | solution.py:377
  51.6 2.0 %collective-permute-done.12 = f32[288,128]{1,0:T(8,128)S(1)} collective-permute-done((f32[288,128]{1,0:T(8,128)S(1)}, f32[288,128]{1,0:T(8,128)S(1)}, u32[]{:S(2)}, u32[]{:S(2)}) %collective-permute-start.12) | collective-permute-done | bytes 147488 | tf_op jit(solution)/shard_map/ppermute | solution.py:377
  53.7 1.6 %collective-permute-done.15 = f32[288,128]{1,0:T(8,128)S(1)} collective-permute-done((f32[288,128]{1,0:T(8,128)S(1)}, f32[288,128]{1,0:T(8,128)S(1)}, u32[]{:S(2)}, u32[]{:S(2)}) %collective-permute-start.15) | collective-permute-done | bytes 147488 | tf_op jit(solution)/shard_map/ppermute | solution.py:377
  55.4 0.1 collective-permute-start.16
  55.5 1.7 %collective-permute-done.16.refs_2_ = f32[2,384,128]{2,1,0:T(8,128)S(1)} collective-permute-done((f32[2,384,128]{2,1,0:T(8,128)S(1)}, f32[2,384,128]{2,1,0:T(8,128)S(1)}, u32[]{:S(2)}, u32[]{:S(2)}) %collective-permute-start.16) | collective-permute-done | bytes 393248 | tf_op jit(solution)/shard_map/ppermute | solution.py:377
  57.2 13.6 %shard_map.40 = f32[2048,384]{1,0:T(8,128)} custom-call(s32[1]{0:T(128)} %bitcast.core_ref.refs_0_, f32[2,384,128]{2,1,0:T(8,128)S(1)} %pad_maximum_fusion.refs_1_, f32[2,384,128]{2,1,0:T(8,128)S(1)} %collective-permute-done.16.refs_2_, f32[2048,256]{1,0:T(8,128)} %refs_3_.1, f32[2048,128]{1,0:T(8,128)} %refs_4_.1), custom_call_target="tpu_custom_call" | custom-call | tf_op jit(solution)/shard_map/pallas_call | solution.py:351
  (30 shorter events, 0.5 us)
Async XLA Ops:
  6.3 5.2 %collective-permute-start = (f32[4,240,128]{2,1,0:T(8,128)S(1)}, f32[4,240,128]{2,1,0:T(8,128)S(1)}, u32[]{:S(2)}, u32[]{:S(2)}) collective-permute-start(f32[4,240,128]{2,1,0:T(8,128)S(1)} %get-tuple-element.18), channel_id=1, source_target_pairs={{0,1},{1,0},{2,3},{3,2},{4,5},{5,4},{6,7},{7,6},{8,9},{9,8},{10,11... | collective-permute-start | bytes 1474568 | tf_op jit(solution)/shard_map/ppermute | solution.py:377
  6.9 7.7 %collective-permute-start.5 = (f32[4,240,128]{2,1,0:T(8,128)S(1)}, f32[4,240,128]{2,1,0:T(8,128)S(1)}, u32[]{:S(2)}, u32[]{:S(2)}) collective-permute-start(f32[4,240,128]{2,1,0:T(8,128)S(1)} %get-tuple-element.20), channel_id=1, source_target_pairs={{0,1},{1,0},{2,3},{3,2},{4,5},{5,4},{6,7},{7,6},{8,9},{9,8},{10,11... | collective-permute-start | bytes 1474568 | tf_op jit(solution)/shard_map/ppermute | solution.py:377
  11.5 9.2 %collective-permute-start.1 = (f32[2,240,128]{2,1,0:T(8,128)S(1)}, f32[2,240,128]{2,1,0:T(8,128)S(1)}, u32[]{:S(2)}, u32[]{:S(2)}) collective-permute-start(f32[2,240,128]{2,1,0:T(8,128)S(1)} %add_bitcast_fusion.1), channel_id=1, source_target_pairs={{0,2},{1,3},{2,0},{3,1},{4,6},{5,7},{6,4},{7,5},{8,10},{9,11},{10,... | collective-permute-start | bytes 737288 | tf_op jit(solution)/shard_map/ppermute | solution.py:377
  14.6 8.0 %collective-permute-start.6 = (f32[2,240,128]{2,1,0:T(8,128)S(1)}, f32[2,240,128]{2,1,0:T(8,128)S(1)}, u32[]{:S(2)}, u32[]{:S(2)}) collective-permute-start(f32[2,240,128]{2,1,0:T(8,128)S(1)} %add_bitcast_fusion), channel_id=1, source_target_pairs={{0,4},{4,0},{8,12},{12,8},{16,20},{20,16},{24,28},{28,24},{1,5},{5... | collective-permute-start | bytes 737288 | tf_op jit(solution)/shard_map/ppermute | solution.py:377
  20.8 4.9 %collective-permute-start.2 = (f32[240,128]{1,0:T(8,128)S(1)}, f32[240,128]{1,0:T(8,128)S(1)}, u32[]{:S(2)}, u32[]{:S(2)}) collective-permute-start(f32[240,128]{1,0:T(8,128)S(1)} %bitcast_add_fusion.2), channel_id=1, source_target_pairs={{0,4},{4,0},{8,12},{12,8},{16,20},{20,16},{24,28},{28,24},{1,5},{5... | collective-permute-start | bytes 368648 | tf_op jit(solution)/shard_map/ppermute | solution.py:377
  22.6 5.0 %collective-permute-start.7 = (f32[240,128]{1,0:T(8,128)S(1)}, f32[240,128]{1,0:T(8,128)S(1)}, u32[]{:S(2)}, u32[]{:S(2)}) collective-permute-start(f32[240,128]{1,0:T(8,128)S(1)} %bitcast_add_fusion), channel_id=1, source_target_pairs={{0,2},{1,3},{2,0},{3,1},{4,6},{5,7},{6,4},{7,5},{8,10},{9,11},{10,... | collective-permute-start | bytes 368648 | tf_op jit(solution)/shard_map/ppermute | solution.py:377
  25.7 6.3 %collective-permute-start.3 = (f32[240,128]{1,0:T(8,128)S(1)}, f32[240,128]{1,0:T(8,128)S(1)}, u32[]{:S(2)}, u32[]{:S(2)}) collective-permute-start(f32[240,128]{1,0:T(8,128)S(1)} %fusion.1), channel_id=1, source_target_pairs={{0,8},{4,12},{8,0},{12,4},{16,24},{20,28},{24,16},{28,20},{1,9},{5... | collective-permute-start | bytes 368648 | tf_op jit(solution)/shard_map/ppermute | solution.py:377
  27.6 8.3 %collective-permute-start.8 = (f32[240,128]{1,0:T(8,128)S(1)}, f32[240,128]{1,0:T(8,128)S(1)}, u32[]{:S(2)}, u32[]{:S(2)}) collective-permute-start(f32[240,128]{1,0:T(8,128)S(1)} %fusion), channel_id=1, source_target_pairs={{0,24},{4,28},{8,16},{12,20},{16,8},{20,12},{24,0},{28,4},{1,25},{... | collective-permute-start | bytes 368648 | tf_op jit(solution)/shard_map/ppermute | solution.py:377
  32.0 7.2 %collective-permute-start.4 = (f32[240,128]{1,0:T(8,128)S(1)}, f32[240,128]{1,0:T(8,128)S(1)}, u32[]{:S(2)}, u32[]{:S(2)}) collective-permute-start(f32[240,128]{1,0:T(8,128)S(1)} %add.160.a_ref), channel_id=1, source_target_pairs={{0,24},{4,28},{8,16},{12,20},{16,8},{20,12},{24,0},{28,4},{1,25},{... | collective-permute-start | bytes 368648 | tf_op jit(solution)/shard_map/ppermute | solution.py:377
  35.9 4.9 %collective-permute-start.9 = (f32[240,128]{1,0:T(8,128)S(1)}, f32[240,128]{1,0:T(8,128)S(1)}, u32[]{:S(2)}, u32[]{:S(2)}) collective-permute-start(f32[240,128]{1,0:T(8,128)S(1)} %add.170.b_ref), channel_id=1, source_target_pairs={{0,8},{4,12},{8,0},{12,4},{16,24},{20,28},{24,16},{28,20},{1,9},{5... | collective-permute-start | bytes 368648 | tf_op jit(solution)/shard_map/ppermute | solution.py:377
  41.5 1.4 %collective-permute-start.10 = (f32[192,128]{1,0:T(8,128)S(1)}, f32[192,128]{1,0:T(8,128)S(1)}, u32[]{:S(2)}, u32[]{:S(2)}) collective-permute-start(f32[192,128]{1,0:T(8,128)S(1)} %get-tuple-element.22), channel_id=1, source_target_pairs={{0,1},{1,0},{2,3},{3,2},{4,5},{5,4},{6,7},{7,6},{8,9},{9,8},{10,11... | collective-permute-start | bytes 294920 | tf_op jit(solution)/shard_map/ppermute | solution.py:377
  41.6 2.9 %collective-permute-start.13 = (f32[192,128]{1,0:T(8,128)S(1)}, f32[192,128]{1,0:T(8,128)S(1)}, u32[]{:S(2)}, u32[]{:S(2)}) collective-permute-start(f32[192,128]{1,0:T(8,128)S(1)} %get-tuple-element.25), channel_id=1, source_target_pairs={{0,1},{1,0},{2,3},{3,2},{4,5},{5,4},{6,7},{7,6},{8,9},{9,8},{10,11... | collective-permute-start | bytes 294920 | tf_op jit(solution)/shard_map/ppermute | solution.py:377
  42.9 5.4 %collective-permute-start.11 = (f32[240,128]{1,0:T(8,128)S(1)}, f32[240,128]{1,0:T(8,128)S(1)}, u32[]{:S(2)}, u32[]{:S(2)}) collective-permute-start(f32[240,128]{1,0:T(8,128)S(1)} %pad_maximum_fusion.3), channel_id=1, source_target_pairs={{0,2},{1,3},{2,0},{3,1},{4,6},{5,7},{6,4},{7,5},{8,10},{9,11},{10,... | collective-permute-start | bytes 368648 | tf_op jit(solution)/shard_map/ppermute | solution.py:377
  44.5 5.5 %collective-permute-start.14 = (f32[240,128]{1,0:T(8,128)S(1)}, f32[240,128]{1,0:T(8,128)S(1)}, u32[]{:S(2)}, u32[]{:S(2)}) collective-permute-start(f32[240,128]{1,0:T(8,128)S(1)} %pad_maximum_fusion.4), channel_id=1, source_target_pairs={{0,4},{4,0},{8,12},{12,8},{16,20},{20,16},{24,28},{28,24},{1,5},{5... | collective-permute-start | bytes 368648 | tf_op jit(solution)/shard_map/ppermute | solution.py:377
  48.4 5.2 %collective-permute-start.12 = (f32[288,128]{1,0:T(8,128)S(1)}, f32[288,128]{1,0:T(8,128)S(1)}, u32[]{:S(2)}, u32[]{:S(2)}) collective-permute-start(f32[288,128]{1,0:T(8,128)S(1)} %pad_maximum_fusion.1), channel_id=1, source_target_pairs={{0,4},{4,0},{8,12},{12,8},{16,20},{20,16},{24,28},{28,24},{1,5},{5... | collective-permute-start | bytes 442376 | tf_op jit(solution)/shard_map/ppermute | solution.py:377
  50.1 5.2 %collective-permute-start.15 = (f32[288,128]{1,0:T(8,128)S(1)}, f32[288,128]{1,0:T(8,128)S(1)}, u32[]{:S(2)}, u32[]{:S(2)}) collective-permute-start(f32[288,128]{1,0:T(8,128)S(1)} %pad_maximum_fusion.2), channel_id=1, source_target_pairs={{0,2},{1,3},{2,0},{3,1},{4,6},{5,7},{6,4},{7,5},{8,10},{9,11},{10,... | collective-permute-start | bytes 442376 | tf_op jit(solution)/shard_map/ppermute | solution.py:377
  55.4 1.8 %collective-permute-start.16 = (f32[2,384,128]{2,1,0:T(8,128)S(1)}, f32[2,384,128]{2,1,0:T(8,128)S(1)}, u32[]{:S(2)}, u32[]{:S(2)}) collective-permute-start(f32[2,384,128]{2,1,0:T(8,128)S(1)} %pad_maximum_fusion.refs_1_), channel_id=1, source_target_pairs={{0,1},{1,0},{2,3},{3,2},{4,5},{5,4},{6,7},{7,6},{8,9},{9,8},{10,11... | collective-permute-start | bytes 1179656 | tf_op jit(solution)/shard_map/ppermute | solution.py:377

commit v3 on v2

--- a/solution.py
+++ b/solution.py
@@ -13,6 +13,7 @@
 BLOCK = 16
 PANEL = 2
 CHUNKS = 4
+SHARE = 9
 LIMIT = pltpu.CompilerParams(vmem_limit_bytes=32 << 20)
 VMEM = pltpu.VMEM
 
@@ -120,7 +121,8 @@
     obs = jacobian.shape[1]
     tiles = wide // LANES
     packed = tiles * (tiles + 1) // 2 * LANES // 8
-    sums = VMEM((4, (wide + packed) // 2, obs // 8), F32)
+    cut = (wide + packed) * SHARE // 20
+    sums = [VMEM((4, size, obs // 8), F32) for size in (cut, wide + packed - cut)]
     own = VMEM((4 * packed, obs // 8), F32)
     inside = pl.BlockSpec(memory_space=VMEM)
     outside = pl.BlockSpec(memory_space=pltpu.HBM)
@@ -131,7 +133,7 @@
             functools.partial(products_kernel, first),
             in_specs=[scalar, outside, outside, outside] + [inside] * len(more),
             out_specs=[inside] * (3 if first else 2),
-            out_shape=[sums, sums, own] if first else [sums, sums],
+            out_shape=[*sums, own] if first else sums,
             scratch_shapes=[
                 VMEM((rows, wide), F32),
                 VMEM((rows, obs // 2), F32),
@@ -247,7 +249,7 @@
     inside = pl.BlockSpec(memory_space=VMEM)
     tiles = wide // LANES
     part = VMEM((tiles * (tiles + 1) * LANES // 8, LANES), F32)
-    gram = VMEM(((2 * a.shape[0] - wide) // 2, LANES), F32)
+    gram = VMEM(((a.shape[0] + b.shape[0] - wide) // 2, LANES), F32)
     return pl.pallas_call(
         hess_kernel,
         in_specs=[pl.BlockSpec(memory_space=pltpu.SMEM)] + [inside] * 4,
@@ -392,7 +394,7 @@
     )
     mine, theirs = products(core, basis, new_vectors, jacobian)
     a, b = (value.reshape(2, 2, *value.shape[1:]) for value in mine)
-    up_a, up_b = (swap(value, "cols", 1).reshape(a.shape) for value in theirs)
+    up_a, up_b = (swap(value, "cols", 1).reshape(2, 2, *value.shape[1:]) for value in theirs)
 
     def across(value, index):
         return lax.dynamic_index_in_dim(value, index, 1, keepdims=False)

time: 71.1 us -> 73.2 us (1.030)
  waiting for transfers between devices: 18.3 us -> 24.2 us
  starting transfers between devices: 26.7 us -> 22.9 us
    ppermute x17, waiting for transfers between devices: 18.3 us -> 24.2 us  [swap(): return lax.ppermute(value, axis, [(i, i ^ mask) for i in range(size)])]
    ppermute x17, starting transfers between devices: 26.7 us -> 22.9 us  [swap(): return lax.ppermute(value, axis, [(i, i ^ mask) for i in range(size)])]
  transfers between devices with their start and end apart: 17 -> 17, of which waited for: 10 -> 10; matrix products, arithmetic and copies ran while one was open for 1% -> 0% of each run, Pallas kernels for 6% -> 6%
where the time goes in v3:
time: 73.2 us; the launch traced here: 73 us
  Pallas kernels  25 us (34%)
  waiting for transfers between devices  24.2 us (33%)
  starting transfers between devices  22.9 us (31%)
    ppermute x17, waiting for transfers between devices, swap(): return lax.ppermute(value, axis, [(i, i ^ mask) for i in range(size)])  24.2 us
    ppermute x17, starting transfers between devices, swap(): return lax.ppermute(value, axis, [(i, i ^ mask) for i in range(size)])  22.9 us
    pallas_call x1, Pallas kernels, whiten(): pl.pallas_call(kernel, in_specs=[pl.BlockSpec(memory_space=pltpu.SMEM), i...  13.6 us
    pallas_call x2, Pallas kernels, call(): pl.pallas_call(functools.partial(products_kernel, first), in_specs=[scala...  10.8 us
  transfers between devices with their start and end apart: 17, of which 10 were waited for; matrix products, arithmetic and copies ran while one was open for 0% of the time, Pallas kernels for 6%

profile of v3, /device:TPU:0, one launch (start us, length us, event | category | flops | bytes accessed | tf_op | source)
XLA Modules:
  0.0 73.0 jit_solution(2295444936470400537)
XLA Ops:
  0.0 6.3 %shard_map.37 = (f32[4,216,128]{2,1,0:T(8,128)S(1)}, f32[4,264,128]{2,1,0:T(8,128)S(1)}, f32[384,128]{1,0:T(8,128)S(1)}) custom-call(s32[1]{0:T(128)} %bitcast.core_ref.refs_0_, f32[2048,256]{1,0:T(8,128)} %refs_3_.1, f32[2048,128]{1,0:T(8,128)} %refs_4_.1, f32[2048,1024]{1,0:T(8,128)} %jac_ref.3), custom_call_target="tpu_custom_call" | custom-call | tf_op jit(solution)/shard_map/pallas_call | solution.py:132
  6.3 0.6 collective-permute-start.5
  6.9 0.1 collective-permute-start
  7.0 4.5 %shard_map.38 = (f32[4,216,128]{2,1,0:T(8,128)S(1)}, f32[4,264,128]{2,1,0:T(8,128)S(1)}) custom-call(s32[1]{0:T(128)} %bitcast.core_ref.refs_0_, f32[2048,256]{1,0:T(8,128)} %refs_3_.1, f32[2048,128]{1,0:T(8,128)} %refs_4_.1, f32[2048,1024]{1,0:T(8,128)} %jac_ref.3, f32[384,128]{1,0:T(8,128)S(1)} %get-tuple-element.16.refs_0_), custom_call_target="tpu_custom_call" | custom-call | tf_op jit(solution)/shard_map/pallas_call | solution.py:132
  11.5 0.0 collective-permute-done.5
  11.5 3.0 %collective-permute-start.6 = (f32[2,264,128]{2,1,0:T(8,128)S(1)}, f32[2,264,128]{2,1,0:T(8,128)S(1)}, u32[]{:S(2)}, u32[]{:S(2)}) collective-permute-start(f32[2,264,128]{2,1,0:T(8,128)S(1)} %add_bitcast_fusion), channel_id=1, source_target_pairs={{0,4},{4,0},{8,12},{12,8},{16,20},{20,16},{24,28},{28,24},{1,5},{5... | collective-permute-start | bytes 811016 | tf_op jit(solution)/shard_map/ppermute | solution.py:379
  14.5 0.0 collective-permute-done
  14.5 1.6 %collective-permute-start.1 = (f32[2,216,128]{2,1,0:T(8,128)S(1)}, f32[2,216,128]{2,1,0:T(8,128)S(1)}, u32[]{:S(2)}, u32[]{:S(2)}) collective-permute-start(f32[2,216,128]{2,1,0:T(8,128)S(1)} %add_bitcast_fusion.1), channel_id=1, source_target_pairs={{0,2},{1,3},{2,0},{3,1},{4,6},{5,7},{6,4},{7,5},{8,10},{9,11},{10,... | collective-permute-start | bytes 663560 | tf_op jit(solution)/shard_map/ppermute | solution.py:379
  16.1 5.1 %collective-permute-done.6 = f32[2,264,128]{2,1,0:T(8,128)S(1)} collective-permute-done((f32[2,264,128]{2,1,0:T(8,128)S(1)}, f32[2,264,128]{2,1,0:T(8,128)S(1)}, u32[]{:S(2)}, u32[]{:S(2)}) %collective-permute-start.6) | collective-permute-done | bytes 270368 | tf_op jit(solution)/shard_map/ppermute | solution.py:379
  21.3 1.8 %collective-permute-start.7 = (f32[264,128]{1,0:T(8,128)S(1)}, f32[264,128]{1,0:T(8,128)S(1)}, u32[]{:S(2)}, u32[]{:S(2)}) collective-permute-start(f32[264,128]{1,0:T(8,128)S(1)} %bitcast_add_fusion), channel_id=1, source_target_pairs={{0,2},{1,3},{2,0},{3,1},{4,6},{5,7},{6,4},{7,5},{8,10},{9,11},{10,... | collective-permute-start | bytes 405512 | tf_op jit(solution)/shard_map/ppermute | solution.py:379
  23.1 0.0 collective-permute-done.1
  23.1 1.6 %collective-permute-start.2 = (f32[216,128]{1,0:T(8,128)S(1)}, f32[216,128]{1,0:T(8,128)S(1)}, u32[]{:S(2)}, u32[]{:S(2)}) collective-permute-start(f32[216,128]{1,0:T(8,128)S(1)} %bitcast_add_fusion.2), channel_id=1, source_target_pairs={{0,4},{4,0},{8,12},{12,8},{16,20},{20,16},{24,28},{28,24},{1,5},{5... | collective-permute-start | bytes 331784 | tf_op jit(solution)/shard_map/ppermute | solution.py:379
  24.7 1.7 %collective-permute-done.7 = f32[264,128]{1,0:T(8,128)S(1)} collective-permute-done((f32[264,128]{1,0:T(8,128)S(1)}, f32[264,128]{1,0:T(8,128)S(1)}, u32[]{:S(2)}, u32[]{:S(2)}) %collective-permute-start.7) | collective-permute-done | bytes 135200 | tf_op jit(solution)/shard_map/ppermute | solution.py:379
  26.4 3.9 %collective-permute-start.8 = (f32[264,128]{1,0:T(8,128)S(1)}, f32[264,128]{1,0:T(8,128)S(1)}, u32[]{:S(2)}, u32[]{:S(2)}) collective-permute-start(f32[264,128]{1,0:T(8,128)S(1)} %fusion), channel_id=1, source_target_pairs={{0,24},{4,28},{8,16},{12,20},{16,8},{20,12},{24,0},{28,4},{1,25},{... | collective-permute-start | bytes 405512 | tf_op jit(solution)/shard_map/ppermute | solution.py:379
  30.3 0.0 collective-permute-done.2
  30.3 0.1 collective-permute-start.3
  30.4 3.4 %collective-permute-done.8 = f32[264,128]{1,0:T(8,128)S(1)} collective-permute-done((f32[264,128]{1,0:T(8,128)S(1)}, f32[264,128]{1,0:T(8,128)S(1)}, u32[]{:S(2)}, u32[]{:S(2)}) %collective-permute-start.8) | collective-permute-done | bytes 135200 | tf_op jit(solution)/shard_map/ppermute | solution.py:379
  33.8 1.0 %collective-permute-start.9 = (f32[264,128]{1,0:T(8,128)S(1)}, f32[264,128]{1,0:T(8,128)S(1)}, u32[]{:S(2)}, u32[]{:S(2)}) collective-permute-start(f32[264,128]{1,0:T(8,128)S(1)} %add.172.b_ref), channel_id=1, source_target_pairs={{0,8},{4,12},{8,0},{12,4},{16,24},{20,28},{24,16},{28,20},{1,9},{5... | collective-permute-start | bytes 405512 | tf_op jit(solution)/shard_map/ppermute | solution.py:379
  34.8 1.3 %collective-permute-done.3 = f32[216,128]{1,0:T(8,128)S(1)} collective-permute-done((f32[216,128]{1,0:T(8,128)S(1)}, f32[216,128]{1,0:T(8,128)S(1)}, u32[]{:S(2)}, u32[]{:S(2)}) %collective-permute-start.3) | collective-permute-done | bytes 110624 | tf_op jit(solution)/shard_map/ppermute | solution.py:379
  36.1 2.2 %collective-permute-start.4 = (f32[216,128]{1,0:T(8,128)S(1)}, f32[216,128]{1,0:T(8,128)S(1)}, u32[]{:S(2)}, u32[]{:S(2)}) collective-permute-start(f32[216,128]{1,0:T(8,128)S(1)} %add.162.a_ref), channel_id=1, source_target_pairs={{0,24},{4,28},{8,16},{12,20},{16,8},{20,12},{24,0},{28,4},{1,25},{... | collective-permute-start | bytes 331784 | tf_op jit(solution)/shard_map/ppermute | solution.py:379
  38.3 4.6 %collective-permute-done.4.got_a_ref = f32[216,128]{1,0:T(8,128)S(1)} collective-permute-done((f32[216,128]{1,0:T(8,128)S(1)}, f32[216,128]{1,0:T(8,128)S(1)}, u32[]{:S(2)}, u32[]{:S(2)}) %collective-permute-start.4) | collective-permute-done | bytes 110624 | tf_op jit(solution)/shard_map/ppermute | solution.py:379
  42.8 0.0 collective-permute-done.9.got_b_ref
  42.8 0.6 shard_map.39
  43.5 0.1 collective-permute-start.10
  43.6 0.5 collective-permute-start.13
  44.1 0.8 %collective-permute-done.10 = f32[192,128]{1,0:T(8,128)S(1)} collective-permute-done((f32[192,128]{1,0:T(8,128)S(1)}, f32[192,128]{1,0:T(8,128)S(1)}, u32[]{:S(2)}, u32[]{:S(2)}) %collective-permute-start.10) | collective-permute-done | bytes 98336 | tf_op jit(solution)/shard_map/ppermute | solution.py:379
  44.9 1.7 %collective-permute-start.11 = (f32[240,128]{1,0:T(8,128)S(1)}, f32[240,128]{1,0:T(8,128)S(1)}, u32[]{:S(2)}, u32[]{:S(2)}) collective-permute-start(f32[240,128]{1,0:T(8,128)S(1)} %pad_maximum_fusion.3), channel_id=1, source_target_pairs={{0,2},{1,3},{2,0},{3,1},{4,6},{5,7},{6,4},{7,5},{8,10},{9,11},{10,... | collective-permute-start | bytes 368648 | tf_op jit(solution)/shard_map/ppermute | solution.py:379
  46.6 0.0 collective-permute-done.13
  46.6 1.6 %collective-permute-start.14 = (f32[240,128]{1,0:T(8,128)S(1)}, f32[240,128]{1,0:T(8,128)S(1)}, u32[]{:S(2)}, u32[]{:S(2)}) collective-permute-start(f32[240,128]{1,0:T(8,128)S(1)} %pad_maximum_fusion.4), channel_id=1, source_target_pairs={{0,4},{4,0},{8,12},{12,8},{16,20},{20,16},{24,28},{28,24},{1,5},{5... | collective-permute-start | bytes 368648 | tf_op jit(solution)/shard_map/ppermute | solution.py:379
  48.2 2.1 %collective-permute-done.11 = f32[240,128]{1,0:T(8,128)S(1)} collective-permute-done((f32[240,128]{1,0:T(8,128)S(1)}, f32[240,128]{1,0:T(8,128)S(1)}, u32[]{:S(2)}, u32[]{:S(2)}) %collective-permute-start.11) | collective-permute-done | bytes 122912 | tf_op jit(solution)/shard_map/ppermute | solution.py:379
  50.4 1.7 %collective-permute-start.12 = (f32[288,128]{1,0:T(8,128)S(1)}, f32[288,128]{1,0:T(8,128)S(1)}, u32[]{:S(2)}, u32[]{:S(2)}) collective-permute-start(f32[288,128]{1,0:T(8,128)S(1)} %pad_maximum_fusion.1), channel_id=1, source_target_pairs={{0,4},{4,0},{8,12},{12,8},{16,20},{20,16},{24,28},{28,24},{1,5},{5... | collective-permute-start | bytes 442376 | tf_op jit(solution)/shard_map/ppermute | solution.py:379
  52.1 0.0 collective-permute-done.14
  52.2 1.6 %collective-permute-start.15 = (f32[288,128]{1,0:T(8,128)S(1)}, f32[288,128]{1,0:T(8,128)S(1)}, u32[]{:S(2)}, u32[]{:S(2)}) collective-permute-start(f32[288,128]{1,0:T(8,128)S(1)} %pad_maximum_fusion.2), channel_id=1, source_target_pairs={{0,2},{1,3},{2,0},{3,1},{4,6},{5,7},{6,4},{7,5},{8,10},{9,11},{10,... | collective-permute-start | bytes 442376 | tf_op jit(solution)/shard_map/ppermute | solution.py:379
  53.7 1.9 %collective-permute-done.12 = f32[288,128]{1,0:T(8,128)S(1)} collective-permute-done((f32[288,128]{1,0:T(8,128)S(1)}, f32[288,128]{1,0:T(8,128)S(1)}, u32[]{:S(2)}, u32[]{:S(2)}) %collective-permute-start.12) | collective-permute-done | bytes 147488 | tf_op jit(solution)/shard_map/ppermute | solution.py:379
  55.7 1.7 %collective-permute-done.15 = f32[288,128]{1,0:T(8,128)S(1)} collective-permute-done((f32[288,128]{1,0:T(8,128)S(1)}, f32[288,128]{1,0:T(8,128)S(1)}, u32[]{:S(2)}, u32[]{:S(2)}) %collective-permute-start.15) | collective-permute-done | bytes 147488 | tf_op jit(solution)/shard_map/ppermute | solution.py:379
  57.5 0.1 collective-permute-start.16
  57.6 1.7 %collective-permute-done.16.refs_2_ = f32[2,384,128]{2,1,0:T(8,128)S(1)} collective-permute-done((f32[2,384,128]{2,1,0:T(8,128)S(1)}, f32[2,384,128]{2,1,0:T(8,128)S(1)}, u32[]{:S(2)}, u32[]{:S(2)}) %collective-permute-start.16) | collective-permute-done | bytes 393248 | tf_op jit(solution)/shard_map/ppermute | solution.py:379
  59.3 13.6 %shard_map.40 = f32[2048,384]{1,0:T(8,128)} custom-call(s32[1]{0:T(128)} %bitcast.core_ref.refs_0_, f32[2,384,128]{2,1,0:T(8,128)S(1)} %pad_maximum_fusion.refs_1_, f32[2,384,128]{2,1,0:T(8,128)S(1)} %collective-permute-done.16.refs_2_, f32[2048,256]{1,0:T(8,128)} %refs_3_.1, f32[2048,128]{1,0:T(8,128)} %refs_4_.1), custom_call_target="tpu_custom_call" | custom-call | tf_op jit(solution)/shard_map/pallas_call | solution.py:353
  (30 shorter events, 0.4 us)
Async XLA Ops:
  6.3 5.2 %collective-permute-start.5 = (f32[4,264,128]{2,1,0:T(8,128)S(1)}, f32[4,264,128]{2,1,0:T(8,128)S(1)}, u32[]{:S(2)}, u32[]{:S(2)}) collective-permute-start(f32[4,264,128]{2,1,0:T(8,128)S(1)} %get-tuple-element.20), channel_id=1, source_target_pairs={{0,1},{1,0},{2,3},{3,2},{4,5},{5,4},{6,7},{7,6},{8,9},{9,8},{10,11... | collective-permute-start | bytes 1622024 | tf_op jit(solution)/shard_map/ppermute | solution.py:379
  6.9 7.6 %collective-permute-start = (f32[4,216,128]{2,1,0:T(8,128)S(1)}, f32[4,216,128]{2,1,0:T(8,128)S(1)}, u32[]{:S(2)}, u32[]{:S(2)}) collective-permute-start(f32[4,216,128]{2,1,0:T(8,128)S(1)} %get-tuple-element.18), channel_id=1, source_target_pairs={{0,1},{1,0},{2,3},{3,2},{4,5},{5,4},{6,7},{7,6},{8,9},{9,8},{10,11... | collective-permute-start | bytes 1327112 | tf_op jit(solution)/shard_map/ppermute | solution.py:379
  11.5 9.7 %collective-permute-start.6 = (f32[2,264,128]{2,1,0:T(8,128)S(1)}, f32[2,264,128]{2,1,0:T(8,128)S(1)}, u32[]{:S(2)}, u32[]{:S(2)}) collective-permute-start(f32[2,264,128]{2,1,0:T(8,128)S(1)} %add_bitcast_fusion), channel_id=1, source_target_pairs={{0,4},{4,0},{8,12},{12,8},{16,20},{20,16},{24,28},{28,24},{1,5},{5... | collective-permute-start | bytes 811016 | tf_op jit(solution)/shard_map/ppermute | solution.py:379
  14.5 8.6 %collective-permute-start.1 = (f32[2,216,128]{2,1,0:T(8,128)S(1)}, f32[2,216,128]{2,1,0:T(8,128)S(1)}, u32[]{:S(2)}, u32[]{:S(2)}) collective-permute-start(f32[2,216,128]{2,1,0:T(8,128)S(1)} %add_bitcast_fusion.1), channel_id=1, source_target_pairs={{0,2},{1,3},{2,0},{3,1},{4,6},{5,7},{6,4},{7,5},{8,10},{9,11},{10,... | collective-permute-start | bytes 663560 | tf_op jit(solution)/shard_map/ppermute | solution.py:379
  21.3 5.1 %collective-permute-start.7 = (f32[264,128]{1,0:T(8,128)S(1)}, f32[264,128]{1,0:T(8,128)S(1)}, u32[]{:S(2)}, u32[]{:S(2)}) collective-permute-start(f32[264,128]{1,0:T(8,128)S(1)} %bitcast_add_fusion), channel_id=1, source_target_pairs={{0,2},{1,3},{2,0},{3,1},{4,6},{5,7},{6,4},{7,5},{8,10},{9,11},{10,... | collective-permute-start | bytes 405512 | tf_op jit(solution)/shard_map/ppermute | solution.py:379
  23.1 7.2 %collective-permute-start.2 = (f32[216,128]{1,0:T(8,128)S(1)}, f32[216,128]{1,0:T(8,128)S(1)}, u32[]{:S(2)}, u32[]{:S(2)}) collective-permute-start(f32[216,128]{1,0:T(8,128)S(1)} %bitcast_add_fusion.2), channel_id=1, source_target_pairs={{0,4},{4,0},{8,12},{12,8},{16,20},{20,16},{24,28},{28,24},{1,5},{5... | collective-permute-start | bytes 331784 | tf_op jit(solution)/shard_map/ppermute | solution.py:379
  26.4 7.4 %collective-permute-start.8 = (f32[264,128]{1,0:T(8,128)S(1)}, f32[264,128]{1,0:T(8,128)S(1)}, u32[]{:S(2)}, u32[]{:S(2)}) collective-permute-start(f32[264,128]{1,0:T(8,128)S(1)} %fusion), channel_id=1, source_target_pairs={{0,24},{4,28},{8,16},{12,20},{16,8},{20,12},{24,0},{28,4},{1,25},{... | collective-permute-start | bytes 405512 | tf_op jit(solution)/shard_map/ppermute | solution.py:379
  30.3 5.8 %collective-permute-start.3 = (f32[216,128]{1,0:T(8,128)S(1)}, f32[216,128]{1,0:T(8,128)S(1)}, u32[]{:S(2)}, u32[]{:S(2)}) collective-permute-start(f32[216,128]{1,0:T(8,128)S(1)} %fusion.1), channel_id=1, source_target_pairs={{0,8},{4,12},{8,0},{12,4},{16,24},{20,28},{24,16},{28,20},{1,9},{5... | collective-permute-start | bytes 331784 | tf_op jit(solution)/shard_map/ppermute | solution.py:379
  33.8 9.0 %collective-permute-start.9 = (f32[264,128]{1,0:T(8,128)S(1)}, f32[264,128]{1,0:T(8,128)S(1)}, u32[]{:S(2)}, u32[]{:S(2)}) collective-permute-start(f32[264,128]{1,0:T(8,128)S(1)} %add.172.b_ref), channel_id=1, source_target_pairs={{0,8},{4,12},{8,0},{12,4},{16,24},{20,28},{24,16},{28,20},{1,9},{5... | collective-permute-start | bytes 405512 | tf_op jit(solution)/shard_map/ppermute | solution.py:379
  36.1 6.7 %collective-permute-start.4 = (f32[216,128]{1,0:T(8,128)S(1)}, f32[216,128]{1,0:T(8,128)S(1)}, u32[]{:S(2)}, u32[]{:S(2)}) collective-permute-start(f32[216,128]{1,0:T(8,128)S(1)} %add.162.a_ref), channel_id=1, source_target_pairs={{0,24},{4,28},{8,16},{12,20},{16,8},{20,12},{24,0},{28,4},{1,25},{... | collective-permute-start | bytes 331784 | tf_op jit(solution)/shard_map/ppermute | solution.py:379
  43.5 1.4 %collective-permute-start.10 = (f32[192,128]{1,0:T(8,128)S(1)}, f32[192,128]{1,0:T(8,128)S(1)}, u32[]{:S(2)}, u32[]{:S(2)}) collective-permute-start(f32[192,128]{1,0:T(8,128)S(1)} %get-tuple-element.22), channel_id=1, source_target_pairs={{0,1},{1,0},{2,3},{3,2},{4,5},{5,4},{6,7},{7,6},{8,9},{9,8},{10,11... | collective-permute-start | bytes 294920 | tf_op jit(solution)/shard_map/ppermute | solution.py:379
  43.6 3.0 %collective-permute-start.13 = (f32[192,128]{1,0:T(8,128)S(1)}, f32[192,128]{1,0:T(8,128)S(1)}, u32[]{:S(2)}, u32[]{:S(2)}) collective-permute-start(f32[192,128]{1,0:T(8,128)S(1)} %get-tuple-element.25), channel_id=1, source_target_pairs={{0,1},{1,0},{2,3},{3,2},{4,5},{5,4},{6,7},{7,6},{8,9},{9,8},{10,11... | collective-permute-start | bytes 294920 | tf_op jit(solution)/shard_map/ppermute | solution.py:379
  44.9 5.4 %collective-permute-start.11 = (f32[240,128]{1,0:T(8,128)S(1)}, f32[240,128]{1,0:T(8,128)S(1)}, u32[]{:S(2)}, u32[]{:S(2)}) collective-permute-start(f32[240,128]{1,0:T(8,128)S(1)} %pad_maximum_fusion.3), channel_id=1, source_target_pairs={{0,2},{1,3},{2,0},{3,1},{4,6},{5,7},{6,4},{7,5},{8,10},{9,11},{10,... | collective-permute-start | bytes 368648 | tf_op jit(solution)/shard_map/ppermute | solution.py:379
  46.6 5.5 %collective-permute-start.14 = (f32[240,128]{1,0:T(8,128)S(1)}, f32[240,128]{1,0:T(8,128)S(1)}, u32[]{:S(2)}, u32[]{:S(2)}) collective-permute-start(f32[240,128]{1,0:T(8,128)S(1)} %pad_maximum_fusion.4), channel_id=1, source_target_pairs={{0,4},{4,0},{8,12},{12,8},{16,20},{20,16},{24,28},{28,24},{1,5},{5... | collective-permute-start | bytes 368648 | tf_op jit(solution)/shard_map/ppermute | solution.py:379
  50.4 5.2 %collective-permute-start.12 = (f32[288,128]{1,0:T(8,128)S(1)}, f32[288,128]{1,0:T(8,128)S(1)}, u32[]{:S(2)}, u32[]{:S(2)}) collective-permute-start(f32[288,128]{1,0:T(8,128)S(1)} %pad_maximum_fusion.1), channel_id=1, source_target_pairs={{0,4},{4,0},{8,12},{12,8},{16,20},{20,16},{24,28},{28,24},{1,5},{5... | collective-permute-start | bytes 442376 | tf_op jit(solution)/shard_map/ppermute | solution.py:379
  52.2 5.2 %collective-permute-start.15 = (f32[288,128]{1,0:T(8,128)S(1)}, f32[288,128]{1,0:T(8,128)S(1)}, u32[]{:S(2)}, u32[]{:S(2)}) collective-permute-start(f32[288,128]{1,0:T(8,128)S(1)} %pad_maximum_fusion.2), channel_id=1, source_target_pairs={{0,2},{1,3},{2,0},{3,1},{4,6},{5,7},{6,4},{7,5},{8,10},{9,11},{10,... | collective-permute-start | bytes 442376 | tf_op jit(solution)/shard_map/ppermute | solution.py:379
  57.5 1.8 %collective-permute-start.16 = (f32[2,384,128]{2,1,0:T(8,128)S(1)}, f32[2,384,128]{2,1,0:T(8,128)S(1)}, u32[]{:S(2)}, u32[]{:S(2)}) collective-permute-start(f32[2,384,128]{2,1,0:T(8,128)S(1)} %pad_maximum_fusion.refs_1_), channel_id=1, source_target_pairs={{0,1},{1,0},{2,3},{3,2},{4,5},{5,4},{6,7},{7,6},{8,9},{9,8},{10,11... | collective-permute-start | bytes 1179656 | tf_op jit(solution)/shard_map/ppermute | solution.py:379
